TPU v7x, 32 devices: a whole 2x2x4 slice. The times are simulated.
32 devices in a mesh: dp: 8 (over y, x, core), branch: 4 (over z).
Axes of the slice: x: 2, y: 2, z: 4, core: 2. Of those that a mesh axis runs over, the one named last changes fastest.
Arguments:
- image_hidden: bfloat16 [4096, 1024], P('dp', 'branch'), may hold values from -8 to 8
- text_hidden: bfloat16 [4096, 768], P('dp', 'branch'), may hold values from -8 to 8
- image_proj: bfloat16 [1024, 768], replicated, may hold values from -0.1875 to 0.1875
- text_proj: bfloat16 [768, 768], replicated, may hold values from -0.21650635 to 0.21650635
- log_inverse_sharpness: float32 [1], replicated, may hold values from 4 to 5.9
- partner: int32 [4096], replicated, may hold values from 0 to 4095, each once
Outputs:
- loss: float32 [1], replicated
- grad_log_scale: float32 [1], replicated
- grad_image_hidden: bfloat16 [4096, 1024], P('dp', 'branch')
- grad_text_hidden: bfloat16 [4096, 768], P('dp', 'branch')
- grad_image_proj: float32 [1024, 768], P('branch')
- grad_text_proj: float32 [768, 768], P('branch')
Inputs may be any that keep to these rules, and one draw needn't show every extreme that they name: `partner`: each text index appears exactly once.
All inputs are finite; a program needn't handle non-finite values.
Results may differ from a plain program's by a relative error of at most 0.0029.
The roundings to bfloat16 on the way count: a program that leaves them out, or rounds other values in their place, can miss the bound.
Values may be sent and summed in bfloat16 or wider, within the bound.
A program may use at most 64 MiB of HBM per device.

v0:
```python
import functools

import jax
import jax.numpy as jnp
from jax import lax
from jax.experimental import pallas as pl
from jax.experimental.pallas import tpu as pltpu
from jax.sharding import PartitionSpec as P

NORM_EPSILON = 1e-06
MESH = pl.DeviceIdType.MESH
VMEM = pltpu.VMEM
BF = jnp.bfloat16
F32 = jnp.float32


def xor(me, r):
    out, bit = me, 1
    while bit <= r:
        if r & bit:
            out = out + bit * (1 - 2 * lax.rem(lax.div(me, bit), 2))
        bit *= 2
    return out


def span(masks):
    held = [0]
    for m in masks:
        held = held + [r ^ m for r in held]
    return held


def orders(count):
    bits = []
    b = 2
    while b < count:
        bits.append(b)
        b *= 2
    return [[1] + bits, [1] + bits[::-1]]


def halves(width):
    return [pl.ds(0, width // 2), pl.ds(width // 2, width - width // 2)]


def send(src, dst, ssem, rsem, axis, peer):
    return pltpu.make_async_remote_copy(
        src_ref=src, dst_ref=dst, send_sem=ssem, recv_sem=rsem, device_id={axis: peer}, device_id_type=MESH
    )


def greet(pairs):
    barrier = pltpu.get_barrier_semaphore()
    for axis, peer in pairs:
        pl.semaphore_signal(barrier, inc=1, device_id={axis: peer}, device_id_type=MESH)
    pl.semaphore_wait(barrier, len(pairs))


def far_first(count):
    bits = [1 << k for k in range(count.bit_length() - 1)][::-1]
    return [bits, bits]


class CubeGather:
    def __init__(self, axis, me, masks, out, ssem, rsem, absolute):
        self.axis, self.me, self.orders, self.out, self.ssem, self.rsem = axis, me, masks, out, ssem, rsem
        self.absolute = absolute
        self.cols = halves(out.shape[2])
        self.arriving, self.sent = [{}, {}], []

    def slot(self, r):
        return xor(self.me, r) if self.absolute else r

    def push(self, i, h, r):
        m = self.orders[h][i]
        self.ready(h, r)
        c = self.cols[h]
        here = self.slot(r)
        there = here if self.absolute else r ^ m
        cp = send(
            self.out.at[here, :, c], self.out.at[there, :, c], self.ssem.at[h, r ^ m], self.rsem.at[h, r ^ m],
            self.axis, xor(self.me, m),
        )
        cp.start()
        self.arriving[h][r ^ m] = cp
        self.sent.append(cp)

    def own(self, h):
        for i in range(self.steps()):
            self.push(i, h, 0)

    def forward(self, i):
        for h in (0, 1):
            for r in span(self.orders[h][:i])[1:]:
                self.push(i, h, r)

    def ready(self, h, r):
        cp = self.arriving[h].pop(r, None)
        if cp is not None:
            cp.wait_recv()

    def steps(self):
        return len(self.orders[0])

    def finish(self):
        for h in (0, 1):
            for r in list(self.arriving[h]):
                self.ready(h, r)
        for cp in self.sent:
            cp.wait_send()


def dp_gather(me, count, out, ssem, rsem, absolute):
    return CubeGather("dp", me, [o[::-1] for o in orders(count)], out, ssem, rsem, absolute)


def branch_gather(me, n, out, ssem, rsem):
    return CubeGather("branch", me, far_first(n), out, ssem, rsem, True)


class CubeReduce:
    def __init__(self, axis, masks, me, count, src, acc, rcv, ssem, rsem, absolute):
        self.axis, self.orders = axis, masks
        self.me, self.count, self.src, self.acc, self.rcv = me, count, src, acc, rcv
        self.ssem, self.rsem, self.absolute = ssem, rsem, absolute
        self.cols = halves(src.shape[2])
        self.live = {}
        self.sent = []

    def steps(self):
        return len(self.orders[0])

    def slot(self, r):
        return xor(self.me, r) if self.absolute else r

    def place(self, h, i, k):
        base = sum(self.count >> (j + 1) for j in range(i))
        return base + sorted(span(self.orders[h][i + 1 :])).index(k)

    def start(self, i, h, r):
        m = self.orders[h][i]
        k = r ^ m
        p = self.place(h, i, k)
        c = self.cols[h]
        src = self.src.at[self.slot(r), :, c] if i == 0 else self.acc.at[r, :, c]
        cp = send(src, self.rcv.at[p, :, c], self.ssem.at[h, p], self.rsem.at[h, p], self.axis, xor(self.me, m))
        cp.start()
        self.live[(h, i, k)] = cp
        self.sent.append(cp)

    def first(self):
        for h in (0, 1):
            m = self.orders[h][0]
            for r in span(self.orders[h]):
                if r & m:
                    self.start(0, h, r)

    def merge(self, i, h):
        c = self.cols[h]
        later = self.orders[h][i + 1] if i + 1 < self.steps() else 0
        for k in sorted(span(self.orders[h][i + 1 :]), key=lambda k: 0 if k & later else 1):
            self.live[(h, i, k)].wait_recv()
            mine = self.src[self.slot(k), :, c] if i == 0 else self.acc[k, :, c]
            self.acc[k, :, c] = mine + self.rcv[self.place(h, i, k), :, c]
            if k & later:
                self.start(i + 1, h, k)

    def finish(self):
        for cp in self.sent:
            cp.wait_send()


def project_kernel(n, count, ih, th, ip, tp, gi, gt, iu, il, tu, tl, ib, tb, s1, r1, s2, r2, s3, r3):
    b, d = lax.axis_index("branch"), lax.axis_index("dp")
    masks = orders(count)[0]
    greet([("branch", xor(b, r)) for r in range(1, n)] + [("dp", xor(d, m)) for m in masks])
    copies = []
    for j, (src, dst) in enumerate(((th, tb), (ih, ib))):
        for r in range(1, n):
            p = xor(b, r)
            cp = send(src.at[p], dst.at[r], s1.at[j, r], r1.at[j, r], "branch", p)
            cp.start()
            copies.append((j, r, cp))

    def project(j, src, dst, proj, unit, length, out_slot):
        raw = jnp.dot(src[b], proj[b], preferred_element_type=F32)
        for jj, r, cp in copies:
            if jj == j:
                cp.wait_recv()
                raw = raw + jnp.dot(dst[r], proj[xor(b, r)], preferred_element_type=F32)
        size = jnp.sqrt(jnp.sum(raw * raw, axis=1, keepdims=True) + NORM_EPSILON)
        u = raw / size
        unit[...] = u
        length[...] = jnp.broadcast_to(size, length.shape)
        out_slot[...] = u.astype(BF)

    project(0, th, tb, tp, tu, tl, gt.at[0])
    gather = dp_gather(d, count, gt, s2, r2, False)
    line = branch_gather(b, n, gi, s3, r3)
    for h in (0, 1):
        gather.own(h)
    project(1, ih, ib, ip, iu, il, gi.at[b])
    for h in (0, 1):
        line.own(h)
    for i in range(1, max(gather.steps(), line.steps())):
        if i < gather.steps():
            gather.forward(i)
        if i < line.steps():
            line.forward(i)
    gather.finish()
    line.finish()
    for _, _, cp in copies:
        cp.wait_send()


def stats_kernel(n, count, rs, cs, row_out, col_out, rb, cb, s1, r1, s2, r2):
    b, d = lax.axis_index("branch"), lax.axis_index("dp")
    greet([("branch", xor(b, r)) for r in range(1, n)] + [("dp", xor(d, m)) for m in range(1, count)])
    rows, columns = [], []
    for m in range(1, count):
        cp = send(cs, cb.at[m], s2.at[m], r2.at[m], "dp", xor(d, m))
        cp.start()
        columns.append(cp)
    for r in range(1, n):
        cp = send(rs, rb.at[r], s1.at[r], r1.at[r], "branch", xor(b, r))
        cp.start()
        rows.append(cp)
    for cp in rows:
        cp.wait()
    peak = rs[0]
    for r in range(1, n):
        peak = jnp.maximum(peak, rb[r, 0])
    mass = rs[1] * jnp.exp(rs[0] - peak)
    positive = rs[2]
    for r in range(1, n):
        mass = mass + rb[r, 1] * jnp.exp(rb[r, 0] - peak)
        positive = positive + rb[r, 2]
    row_out[0] = peak + jnp.log(mass)
    row_out[1] = positive
    for cp in columns:
        cp.wait()
    for k in range(count):
        peak = cs[0, k]
        for m in range(1, count):
            peak = jnp.maximum(peak, cb[m, 0, k ^ m])
        mass = cs[1, k] * jnp.exp(cs[0, k] - peak)
        for m in range(1, count):
            mass = mass + cb[m, 1, k ^ m] * jnp.exp(cb[m, 0, k ^ m] - peak)
        col_out[k] = peak + jnp.log(mass)


def grads_kernel(
    n, count, ipart, tpart, iu, il, tu, tl, sc, gi, gt, sc_out,
    iacc, irb, acc, trb, scb, s1, r1, s2, r2, s3, r3, s4, r4, s5, r5,
):
    b, d = lax.axis_index("branch"), lax.axis_index("dp")
    masks = orders(count)[0]
    greet([("branch", xor(b, r)) for r in range(1, n)] + [("dp", xor(d, m)) for m in masks])
    text = CubeReduce("dp", orders(count), d, count, tpart, acc, trb, s2, r2, False)
    text.first()
    near = [o[::-1] for o in far_first(n)]
    image = CubeReduce("branch", near, b, n, ipart, iacc, irb, s1, r1, True)
    image.first()
    scal = []
    for r in range(1, n):
        cp = send(sc, scb.at[r], s4.at[r], r4.at[r], "branch", xor(b, r))
        cp.start()
        scal.append(cp)
    image_line = branch_gather(b, n, gi, s3, r3)
    text_line = branch_gather(b, n, gt, s5, r5)

    def finish_side(line, up, unit, length, out):
        u = unit[...]
        radial = jnp.sum(up * u, axis=1, keepdims=True)
        out[b] = ((up - u * radial) / length[:, 0:1]).astype(BF)
        for h in (0, 1):
            line.own(h)

    for i in range(text.steps()):
        for h in (0, 1):
            text.merge(i, h)
    for i in range(image.steps()):
        for h in (0, 1):
            image.merge(i, h)
        if i == 0:
            finish_side(text_line, acc[0], tu, tl, gt)
    finish_side(image_line, iacc[0], iu, il, gi)
    for line in (text_line, image_line):
        for i in range(1, line.steps()):
            line.forward(i)
    total = sc[...]
    for r in range(1, n):
        scal[r - 1].wait()
        total = total + scb[r]
    sc_out[...] = total
    text.finish()
    image.finish()
    image_line.finish()
    text_line.finish()


def weight_kernel(n, count, wi, wt, sc, oi, ot, sc_out, ai, at, ri, rt, scb, s1, r1, s2, r2, s3, r3, s4, r4, s5, r5):
    d = lax.axis_index("dp")
    greet([("dp", xor(d, m)) for m in range(1, count)])
    reds = [
        CubeReduce("dp", orders(count), d, count, wi, ai, ri, s1, r1, True),
        CubeReduce("dp", orders(count), d, count, wt, at, rt, s4, r4, True),
    ]
    for red in reds:
        red.first()
    scal = []
    for m in range(1, count):
        cp = send(sc, scb.at[m], s3.at[m], r3.at[m], "dp", xor(d, m))
        cp.start()
        scal.append(cp)
    gathers = [dp_gather(d, count, oi, s2, r2, True), dp_gather(d, count, ot, s5, r5, True)]
    for i in range(reds[0].steps()):
        for red, gather in zip(reds, gathers):
            for h in (0, 1):
                red.merge(i, h)
                if i == red.steps() - 1:
                    c = red.cols[h]
                    gather.out[d, :, c] = red.acc[0, :, c]
                    gather.own(h)
    for i in range(1, gathers[0].steps()):
        for gather in gathers:
            gather.forward(i)
    total = sc[...]
    for m in range(1, count):
        scal[m - 1].wait()
        total = total + scb[m]
    sc_out[...] = total
    for part in gathers + reds:
        part.finish()


def call(body, outs, scratch, args, cid):
    spec = pl.BlockSpec(memory_space=VMEM)
    return pl.pallas_call(
        body,
        out_shape=[jax.ShapeDtypeStruct(s, t) for s, t in outs],
        in_specs=[spec] * len(args),
        out_specs=[spec] * len(outs),
        scratch_shapes=scratch,
        compiler_params=pltpu.CompilerParams(
            collective_id=cid, has_side_effects=True, vmem_limit_bytes=60 * 1024 * 1024
        ),
    )(*args)


def per_device(image_hidden, text_hidden, image_proj, text_proj, log_inverse_sharpness, partner):
    n = lax.axis_size("branch")
    count = lax.axis_size("dp")
    branch_pos = lax.axis_index("branch")
    data_pos = lax.axis_index("dp")
    group_rows, image_cols = image_hidden.shape
    text_cols = text_hidden.shape[1]
    own = group_rows // n
    embed = image_proj.shape[1]
    total_pairs = group_rows * count
    denominator = 2.0 * total_pairs
    dma = pltpu.SemaphoreType.DMA
    scale = jnp.exp(log_inverse_sharpness[0])

    group_emb, text_emb, iu, il, tu, tl = call(
        functools.partial(project_kernel, n, count),
        [((n, own, embed), BF), ((count, own, embed), BF), ((own, embed), F32), ((own, 128), F32),
         ((own, embed), F32), ((own, 128), F32)],
        [VMEM((n, own, image_cols), BF), VMEM((n, own, text_cols), BF), dma((2, n)), dma((2, n)),
         dma((2, count)), dma((2, count)), dma((2, n)), dma((2, n))],
        (image_hidden.reshape(n, own, image_cols), text_hidden.reshape(n, own, text_cols),
         image_proj.reshape(n, image_cols, embed), text_proj.reshape(n, text_cols, embed)),
        0,
    )
    group_emb = group_emb.reshape(group_rows, embed)
    text_emb = text_emb.reshape(count * own, embed)

    logits = scale * lax.dot_general(
        group_emb, text_emb, (((1,), (1,)), ((), ())), preferred_element_type=F32
    )
    row_partner = lax.dynamic_slice_in_dim(partner, data_pos * group_rows, group_rows, 0)
    blocks = jnp.bitwise_xor(jnp.arange(count, dtype=jnp.int32), data_pos)
    column_ids = (
        (blocks[:, None] * n + branch_pos) * own + jnp.arange(own, dtype=jnp.int32)[None, :]
    ).reshape(-1)
    matched = row_partner[:, None] == column_ids[None, :]
    positive = jnp.sum(jnp.where(matched, logits, 0.0), axis=1)
    row_peak = jnp.max(logits, axis=1)
    row_mass = jnp.sum(jnp.exp(logits - row_peak[:, None]), axis=1)
    col_peak = jnp.max(logits, axis=0)
    col_mass = jnp.sum(jnp.exp(logits - col_peak[None, :]), axis=0)
    rs = jnp.stack([row_peak, row_mass, positive]).reshape(3, n, own)
    cs = jnp.stack([col_peak, col_mass]).reshape(2, count, 1, own)
    row_stats, col_lse = call(
        functools.partial(stats_kernel, n, count),
        [((2, n, own), F32), ((count, 1, own), F32)],
        [VMEM((n, 3, n, own), F32), VMEM((count, 2, count, 1, own), F32), dma((n,)), dma((n,)),
         dma((count,)), dma((count,))],
        (rs, cs),
        1,
    )
    row_lse, positive = row_stats[0], row_stats[1]
    own_rows = lax.dynamic_slice_in_dim(row_lse - 2.0 * positive, branch_pos, 1, 0)
    loss_part = (jnp.sum(own_rows) + jnp.sum(col_lse[0])) / denominator
    row_lse = row_lse.reshape(-1)
    col_lse = col_lse.reshape(-1)

    weights = (
        jnp.exp(logits - row_lse[:, None])
        + jnp.exp(logits - col_lse[None, :])
        - 2.0 * matched.astype(F32)
    ) / denominator
    scale_part = jnp.sum(weights * logits)
    low = weights.astype(BF)
    ipart = scale * jnp.dot(low, text_emb, preferred_element_type=F32)
    tpart = scale * lax.dot_general(low, group_emb, (((0,), (0,)), ((), ())), preferred_element_type=F32)
    sc = jnp.concatenate([jnp.full((1, 128), loss_part, F32), jnp.full((1, 128), scale_part, F32)])
    gi, gt, sc = call(
        functools.partial(grads_kernel, n, count),
        [((n, own, embed), BF), ((n, own, embed), BF), ((2, 128), F32)],
        [VMEM((n, own, embed), F32), VMEM((n - 1, own, embed), F32), VMEM((count, own, embed), F32), VMEM((count - 1, own, embed), F32),
         VMEM((n, 2, 128), F32), dma((2, n)), dma((2, n)), dma((2, count)), dma((2, count)),
         dma((2, n)), dma((2, n)), dma((n,)), dma((n,)), dma((2, n)), dma((2, n))],
        (ipart.reshape(n, own, embed), tpart.reshape(count, own, embed), iu, il, tu, tl, sc),
        2,
    )
    gi = gi.reshape(group_rows, embed)
    gt = gt.reshape(group_rows, embed)
    image_weight = lax.dot_general(
        image_hidden, gi, (((0,), (0,)), ((), ())), preferred_element_type=F32
    )
    text_weight = lax.dot_general(
        text_hidden, gt, (((0,), (0,)), ((), ())), preferred_element_type=F32
    )
    image_weight = image_weight.reshape(count, image_cols // count, embed)
    text_weight = text_weight.reshape(count, text_cols // count, embed)
    image_sum, text_sum, sc = call(
        functools.partial(weight_kernel, n, count),
        [(image_weight.shape, F32), (text_weight.shape, F32), ((2, 128), F32)],
        [VMEM(image_weight.shape, F32), VMEM(text_weight.shape, F32),
         VMEM((count - 1,) + image_weight.shape[1:], F32), VMEM((count - 1,) + text_weight.shape[1:], F32),
         VMEM((count, 2, 128), F32), dma((2, count)), dma((2, count)), dma((2, count)), dma((2, count)),
         dma((count,)), dma((count,)), dma((2, count)), dma((2, count)), dma((2, count)), dma((2, count))],
        (image_weight, text_weight, sc),
        3,
    )
    image_slab = lax.dynamic_slice_in_dim(image_proj, branch_pos * image_cols, image_cols, 0)
    text_slab = lax.dynamic_slice_in_dim(text_proj, branch_pos * text_cols, text_cols, 0)
    grad_image_hidden = jnp.dot(gi, image_slab.T, preferred_element_type=F32).astype(BF)
    grad_text_hidden = jnp.dot(gt, text_slab.T, preferred_element_type=F32).astype(BF)
    return (
        sc[0, :1],
        sc[1, :1],
        grad_image_hidden,
        grad_text_hidden,
        image_sum.reshape(image_cols, embed),
        text_sum.reshape(text_cols, embed),
    )


def solution(mesh):
    placed = (P("dp", "branch"), P("dp", "branch"), P(), P(), P(), P())
    return jax.shard_map(
        per_device,
        mesh=mesh,
        in_specs=placed,
        out_specs=(
            P(),
            P(),
            P("dp", "branch"),
            P("dp", "branch"),
            P("branch", None),
            P("branch", None),
        ),
        check_vma=False,
    )
```

profile of v0, /device:TPU:0, one launch (start us, length us, event | category | flops | bytes accessed | tf_op | source)
XLA Modules:
  0.0 168.3 jit_solution(3190244160210808496)
XLA Ops:
  1.3 0.8 dynamic_slice.12
  2.2 1.8 %copy.12 = bf16[512,192]{1,0:T(8,128)(2,1)} copy(bf16[512,192]{0,1:T(8,128)(2,1)} %param.7) | data formatting | bytes 393216 | tf_op args[1]
  3.9 34.6 %shard_map.109 = (bf16[4,128,768]{2,1,0:T(8,128)(2,1)}, bf16[8,128,768]{2,1,0:T(8,128)(2,1)}, f32[128,768]{1,0:T(8,128)}, f32[128,128]{1,0:T(8,128)}, f32[128,768]{1,0:T(8,128)}, /*index=5*/f32[128,128]{1,0:T(8,128)}) custom-call(bf16[4,128,256]{2,1,0:T(8,128)(2,1)} %bitcast.52, bf16[4,128,192]{2,1,0:T(8,128)(2,1)} %bitcast.53, ...), custom_call_target="tpu_custom_call" | custom-call | tf_op jit(solution)/shard_map/pallas_call | solution.py:339
  38.5 2.8 %fusion.11 = (f32[1024]{0:T(1024)S(1)}, f32[512]{0:T(512)S(1)}, f32[512,1024]{1,0:T(8,128)S(1)}) fusion(bf16[512,768]{1,0:T(8,128)(2,1)} %bitcast.66, bf16[1024,768]{1,0:T(8,128)(2,1)} %bitcast.64, f32[]{:T(128)} %bitcast), kind=kOutput, calls=%fused_computation.27 | convolution fusion | flops 806877696 | bytes 4462596 | tf_op jit(solution)/shard_map/dot_general | solution.py:378
  41.3 1.0 exponential_reduce_fusion
  42.3 0.6 pad_maximum_fusion.cs
  42.9 0.6 pad_maximum_fusion.1.rs
  43.5 8.2 %shard_map.110 = (f32[2,4,128]{2,1,0:T(4,128)}, f32[8,1,128]{2,1,0:T(1,128)}) custom-call(f32[3,4,128]{2,1,0:T(4,128)} %pad_maximum_fusion.1.rs, f32[2,8,1,128]{3,2,1,0:T(1,128)} %pad_maximum_fusion.cs), custom_call_target="tpu_custom_call" | custom-call | tf_op jit(solution)/shard_map/pallas_call | solution.py:339
  51.7 0.7 multiply_subtract_fusion
  52.4 2.6 %multiply_reduce_fusion = f32[]{:T(128)} fusion(f32[512,1024]{1,0:T(8,128)S(1)} %get-tuple-element.43, f32[1024]{0:T(1024)} %bitcast.61, f32[512]{0:T(512)S(1)} %get-tuple-element.40, s32[1024]{0:T(1024)S(1)} %add_bitcast_fusion, s32[512]{0:T(512)S(1)} %dynamic_slice.12), kind=kLoop, calls=%fused_computation.5 | loop fusion | flops 4718591 | bytes 2109444 | tf_op jit(solution)/shard_map/reduce_sum | solution.py:413
  54.9 0.6 fusion.8
  56.9 0.7 concatenate.7
  57.5 4.2 %convolution_multiply_fusion.2 = f32[512,768]{1,0:T(8,128)} fusion(bf16[1024,768]{1,0:T(8,128)(2,1)} %bitcast.65, f32[]{:T(128)} %bitcast, f32[512,1024]{1,0:T(8,128)S(1)} %get-tuple-element.43, f32[1024]{0:T(1024)S(1)} %bitcast.62, f32[512]{0:T(512)S(1)} %get-tuple-element.40, s32[1024]{0:T(1024)S(1)} %add_bitcast_fusion, s32[512]{0:T(512)S(1)} %dynamic_slice.12), kind=kOutput, calls=%fused_computation.11 | convolution fusion | flops 809893888 | bytes 5255172 | tf_op jit(solution)/shard_map/dot_general | solution.py:415
  61.7 0.6 concatenate.8.sc
  62.4 3.3 %convolution_multiply_fusion = f32[1024,768]{1,0:T(8,128)} fusion(bf16[512,768]{1,0:T(8,128)(2,1)S(1)} %bitcast.67, f32[]{:T(128)} %bitcast, f32[512,1024]{1,0:T(8,128)S(1)} %get-tuple-element.43, f32[1024]{0:T(1024)S(1)} %bitcast.63, f32[512]{0:T(512)S(1)} %get-tuple-element.40, s32[1024]{0:T(1024)S(1)} %add_bitcast_fusion, s32[512]{0:T(512)S(1)} %dynamic_slice.12), kind=kOutput, calls=%fused_computation.9 | convolution fusion | flops 810287104 | bytes 6041604 | tf_op jit(solution)/shard_map/dot_general | solution.py:416
  65.6 65.4 %shard_map.111 = (bf16[4,128,768]{2,1,0:T(8,128)(2,1)}, bf16[4,128,768]{2,1,0:T(8,128)(2,1)}, f32[2,128]{1,0:T(2,128)}) custom-call(f32[4,128,768]{2,1,0:T(8,128)} %bitcast.51, f32[8,128,768]{2,1,0:T(8,128)} %bitcast.43, f32[128,768]{1,0:T(8,128)} %get-tuple-element.24.iu, f32[128,128]{1,0:T(8,128)} %get-tuple-element.25.il, ...), custom_call_target="tpu_custom_call" | custom-call | tf_op jit(solution)/shard_map/pallas_call | solution.py:339
  131.1 2.4 %convolution_convert_fusion.1 = bf16[512,192]{0,1:T(8,128)(2,1)} fusion(bf16[512,768]{1,0:T(8,128)(2,1)} %bitcast.46, bf16[768,768]{1,0:T(8,128)(2,1)} %param.9, s32[]{:T(128)S(6)} %select_n.20), kind=kOutput, calls=%fused_computation.13 | convolution fusion | flops 151093248 | bytes 1277956 | tf_op jit(solution)/shard_map/dot_general | solution.py:450
  133.5 2.3 %fusion.14 = f32[768,192]{0,1:T(8,128)} fusion(bf16[512,192]{0,1:T(8,128)(2,1)S(1)} %copy-done.2, bf16[512,768]{1,0:T(8,128)(2,1)} %bitcast.47), kind=kOutput, calls=%fused_computation.30 | convolution fusion | flops 150994944 | bytes 1572864 | tf_op jit(solution)/shard_map/dot_general | solution.py:432
  135.7 2.1 %convolution_convert_fusion = bf16[512,256]{1,0:T(8,128)(2,1)} fusion(bf16[512,768]{1,0:T(8,128)(2,1)S(1)} %bitcast.44, bf16[1024,768]{1,0:T(8,128)(2,1)} %param.8, s32[]{:T(128)S(6)} %select_n.19), kind=kOutput, calls=%fused_computation.12 | convolution fusion | flops 201457664 | bytes 1441796 | tf_op jit(solution)/shard_map/dot_general | solution.py:449
  137.8 1.3 fusion.13
  139.1 23.9 %shard_map.112 = (f32[8,32,768]{2,1,0:T(8,128)}, f32[8,24,768]{2,1,0:T(8,128)}, f32[2,128]{1,0:T(2,128)}) custom-call(f32[8,32,768]{2,1,0:T(8,128)} %bitcast.42, f32[8,24,768]{2,1,0:T(8,128)} %bitcast.49, f32[2,128]{1,0:T(2,128)} %get-tuple-element.30.sc), custom_call_target="tpu_custom_call" | custom-call | tf_op jit(solution)/shard_map/pallas_call | solution.py:339
  163.1 1.3 fusion.12
  164.3 2.1 %copy.16 = f32[256,768]{1,0:T(8,128)} copy(f32[256,768]{1,0:T(8,128)} %bitcast.54) | data formatting | bytes 1572864
  166.4 1.9 %copy.17 = f32[192,768]{1,0:T(8,128)} copy(f32[192,768]{1,0:T(8,128)} %bitcast.55) | data formatting | bytes 1179648
  (12 shorter events, 0.1 us)
Async XLA Ops:
  51.7 3.3 %copy-start.3 = (f32[8,1,128]{2,1,0:T(1,128)S(1)}, f32[8,1,128]{2,1,0:T(1,128)}, u32[]{:S(2)}) copy-start(f32[8,1,128]{2,1,0:T(1,128)} %get-tuple-element.23) | copy-start | bytes 12292
  57.5 4.9 %copy-start.4 = (bf16[4,128,768]{2,1,0:T(8,128)(2,1)S(1)}, bf16[4,128,768]{2,1,0:T(8,128)(2,1)}, u32[]{:S(2)}) copy-start(bf16[4,128,768]{2,1,0:T(8,128)(2,1)} %get-tuple-element.20) | copy-start | bytes 2359300
  65.6 67.8 %copy-start.2 = (bf16[512,192]{0,1:T(8,128)(2,1)S(1)}, bf16[512,192]{0,1:T(8,128)(2,1)}, u32[]{:S(2)}) copy-start(bf16[512,192]{0,1:T(8,128)(2,1)} %param.7) | copy-start | bytes 589828
  131.1 4.7 %copy-start = (bf16[4,128,768]{2,1,0:T(8,128)(2,1)S(1)}, bf16[4,128,768]{2,1,0:T(8,128)(2,1)}, u32[]{:S(2)}) copy-start(bf16[4,128,768]{2,1,0:T(8,128)(2,1)} %get-tuple-element.28) | copy-start | bytes 2359300
  131.1 6.8 %copy-start.1 = (bf16[512,256]{1,0:T(8,128)(2,1)S(1)}, bf16[512,256]{1,0:T(8,128)(2,1)}, u32[]{:S(2)}) copy-start(bf16[512,256]{1,0:T(8,128)(2,1)} %param.6) | copy-start | bytes 786436
where the time goes:
time: 169 us; the launch traced here: 168 us
  Pallas kernels  132 us (78%)
  matrix products  18.3 us (11%)
  local copies, waits for them, and re-layouts  9.07 us (5%)
  other arithmetic  6.14 us (4%)
  between operations  2.71 us (2%)
    pallas_call x4, Pallas kernels, call(): pl.pallas_call(body, out_shape=[jax.ShapeDtypeStruct(s, t) for s, t in ou...  132 us
    unnamed x13, local copies, waits for them, and re-layouts  5.77 us
    dot_general x1, matrix products, per_device(): ipart = scale * jnp.dot(low, text_emb, preferred_element_type=F32)  4.21 us

commit v1 on v0

v1 whole, which is shorter than its diff:
```python
import functools

import jax
import jax.numpy as jnp
from jax import lax
from jax.experimental import pallas as pl
from jax.experimental.pallas import tpu as pltpu
from jax.sharding import PartitionSpec as P

NORM_EPSILON = 1e-06
MESH = pl.DeviceIdType.MESH
VMEM = pltpu.VMEM
BF = jnp.bfloat16
F32 = jnp.float32
I16 = jnp.int16
TOP = 32767.0


def xor(me, r):
    out, bit = me, 1
    while bit <= r:
        if r & bit:
            out = out + bit * (1 - 2 * lax.rem(lax.div(me, bit), 2))
        bit *= 2
    return out


def greet(pairs):
    barrier = pltpu.get_barrier_semaphore()
    for axis, peer in pairs:
        pl.semaphore_signal(barrier, inc=1, device_id={axis: peer}, device_id_type=MESH)
    pl.semaphore_wait(barrier, len(pairs))


def nn(a, b):
    return jnp.dot(a, b, preferred_element_type=F32)


def nt(a, b):
    return lax.dot_general(a, b, (((1,), (1,)), ((), ())), preferred_element_type=F32)


def tn(a, b):
    return lax.dot_general(a, b, (((0,), (0,)), ((), ())), preferred_element_type=F32)


def eye(rows):
    return lax.broadcasted_iota(jnp.int32, (rows, rows), 0) == lax.broadcasted_iota(jnp.int32, (rows, rows), 1)


def to_lanes(column, diag):
    return jnp.sum(jnp.where(diag, column, 0.0), axis=0, keepdims=True)


def to_column(lanes, diag):
    return jnp.sum(jnp.where(diag, lanes, 0.0), axis=1, keepdims=True)


def coded(x, axis):
    peak = jnp.maximum(jnp.max(jnp.abs(x), axis=axis, keepdims=True), 1e-33)
    return jnp.round(x * (TOP / peak)).astype(jnp.int32).astype(I16), peak * (1.0 / TOP)


def decoded(x):
    return x.astype(jnp.int32).astype(F32)


class Post:
    def __init__(self, sems):
        self.sems, self.count, self.sent = sems, 0, []

    def __call__(self, src, dst, axis, peer):
        i = self.count
        self.count += 1
        cp = pltpu.make_async_remote_copy(
            src_ref=src, dst_ref=dst, send_sem=self.sems.at[0, i], recv_sem=self.sems.at[1, i],
            device_id={axis: peer}, device_id_type=MESH,
        )
        cp.start()
        self.sent.append(cp)
        return cp

    def finish(self):
        for cp in self.sent:
            cp.wait_send()


def packed_shape(rows, width):
    if width == 192 and rows % 64 == 0:
        return rows + rows // 2, 128
    return rows, width


def step_kernel(
    n, count, total, ih, th, ip, tp, pa, lg,
    oih, oth, wqi, wqt, ws, sc_out,
    xi, xt, iu, il, tu, tl, gi, temb, raw, lt, mx, cst, cb, rst, rb, wl,
    tq, ts, tqr, tsr, iup, crecv, iq, isc, iqr, isr, hx, hy, hxg, hyg, di, dt, dgi, dgt, ghi, ght,
    zqi, zqt, zqir, zqtr, zs, zsr, wpi, wpt, scz, scd, sems,
):
    b, d = lax.axis_index("branch"), lax.axis_index("dp")
    core, chip = lax.rem(d, 2), lax.div(d, 2)
    other = 1 - core
    chips = count // 2
    own, embed, width = ih.shape[1], ip.shape[2], tp.shape[1]
    rows, half = n * own, embed // 2
    mid = rows // 2
    ri, rt = ip.shape[1] // chips, width // chips
    packed = xt.shape[1] != rows
    post = Post(sems)
    diag = eye(own)
    zpeers = [xor(b, r) for r in range(n)]
    dpeers = [xor(d, m) for m in range(count)]
    far = list(range(n - 1, 0, -1))
    outward = list(range(2, count, 2))
    bits = [1 << k for k in range(n.bit_length() - 1)][::-1]

    if packed:
        xt[b, :rows] = th[:, :128]
        xt[b, rows:, :64] = th[:mid, 128:]
        xt[b, rows:, 64:] = th[mid:, 128:]
    else:
        xt[b] = th[...]
    greet([("branch", zpeers[r]) for r in range(1, n)] + [("dp", dpeers[m]) for m in range(1, count)])

    features = {r: post(ih.at[zpeers[r]], xi.at[b], "branch", zpeers[r]) for r in far}
    parts = 2
    prow = xt.shape[1] // parts
    tin = {}

    def text_send(r, m, k):
        piece = xt.at[zpeers[r], pl.ds(k * prow, prow)]
        tin[(r ^ m, k)] = post(piece, piece, "branch", zpeers[m])

    for m in bits:
        for k in range(parts):
            text_send(0, m, k)

    def arrive(r):
        for k in range(parts):
            tin[(r, k)].wait_recv()
            for m in bits:
                if m < (r & -r):
                    text_send(r, m, k)

    def normal(x):
        size = jnp.sqrt(jnp.sum(x * x, axis=1, keepdims=True) + NORM_EPSILON)
        return x / size, size

    def text_part(s):
        if packed:
            main, tail = xt[s, :rows], xt[s, rows:]
            low = tp[s, 128:, :]
            zero = jnp.zeros_like(low)
            y = nn(main, tp[s, :128, :])
            lo = nn(tail, jnp.concatenate([low, zero], axis=0))
            hi = nn(tail, jnp.concatenate([zero, low], axis=0))
            y = y + jnp.concatenate([lo, hi], axis=0)
        else:
            y = nn(xt[s], tp[s])
        return y.reshape(n, own, embed)

    raw[...] = text_part(b)
    xi[b] = ih[b]
    x = nn(ih[b], ip[b])
    for r in far[::-1]:
        features[r].wait_recv()
        x = x + nn(xi[zpeers[r]], ip[zpeers[r]])
    u, size = normal(x)
    iu[...] = u
    il[...] = jnp.broadcast_to(size, il.shape)
    gi[d] = u.astype(BF)
    gin = {m: post(gi.at[d], gi.at[d], "dp", dpeers[m]) for m in outward + [1]}

    arrival = sorted(range(1, n), key=lambda r: (r & 1, bin(r).count("1"), -r))
    for r in arrival:
        if r == 1:
            for m in outward:
                gin[m].wait_recv()
                piece = gi.at[dpeers[m]]
                gin[m ^ 1] = post(piece, piece, "dp", dpeers[1])
        arrive(r)
        raw[...] = raw[...] + text_part(zpeers[r])
    for t in range(n):
        u, _ = normal(raw[t])
        temb[t] = u.astype(BF)
    u, size = normal(raw[b])
    tu[...] = u
    tl[...] = jnp.broadcast_to(size, tl.shape)
    for m in range(1, count, 2):
        gin[m].wait_recv()

    def pair(q):
        return gi[2 * q : 2 * q + 2].reshape(2 * own, embed)

    scale = jnp.exp(lg[...])
    texts = temb[...].reshape(rows, embed)
    for q in range(chips):
        y = scale * nt(texts, pair(q))
        lt[q] = y.reshape(n, own, 2 * own)
        top = jnp.max(y, axis=0, keepdims=True)
        cst[0, q] = top
        cst[1, q] = jnp.sum(jnp.exp(y - top), axis=0, keepdims=True)
        near = jnp.maximum(y[:, :own], y[:, own:])
        mx[...] = near if q == 0 else jnp.maximum(mx[...], near)
    cin = [post(cst, cb.at[m], "dp", dpeers[m]) for m in range(1, count)]
    for t in range(n):
        top = jnp.max(mx[pl.ds(t * own, own)], axis=1, keepdims=True)
        mass = jnp.zeros((own, own), F32)
        for q in range(chips):
            e = jnp.exp(lt[q, t] - top)
            mass = mass + e[:, :own] + e[:, own:]
        rst[0, t] = to_lanes(top, diag)
        rst[1, t] = to_lanes(jnp.sum(mass, axis=1, keepdims=True), diag)
    rin = [post(rst, rb.at[r], "branch", zpeers[r]) for r in far]

    def turned(x):
        return jnp.transpose(x.astype(F32))

    start = pl.multiple_of(b * own, own)
    for s in range(n):
        h = turned(xi[s]).astype(BF)
        for q in range(chips):
            hx[q, s] = h[q * ri : (q + 1) * ri]
        h = turned(xt[s, pl.ds(start, own)])
        if packed:
            tail = turned(xt[s, pl.ds(pl.multiple_of(rows + lax.rem(b, n // 2) * own, own), own)])
            h = jnp.concatenate([h, jnp.where(b < n // 2, tail[:64], tail[64:])], axis=0)
        h = h.astype(BF)
        for q in range(chips):
            hy[q, s] = h[q * rt : (q + 1) * rt]
    hin = []
    for m in range(1, count):
        k = lax.div(dpeers[m], 2)
        hin.append(post(hx.at[k], hxg.at[d], "dp", dpeers[m]))
        hin.append(post(hy.at[k], hyg.at[d], "dp", dpeers[m]))
    hxg[d] = hx[chip]
    hyg[d] = hy[chip]

    def merged(held, came, k, many):
        top = held[0, k]
        for m in range(1, many):
            top = jnp.maximum(top, came[m, 0, k])
        mass = held[1, k] * jnp.exp(held[0, k] - top)
        for m in range(1, many):
            mass = mass + came[m, 1, k] * jnp.exp(came[m, 0, k] - top)
        return top + jnp.log(mass)

    for cp in cin:
        cp.wait_recv()
    ilse = [merged(cst, cb, q, count) for q in range(chips)]
    for cp in rin:
        cp.wait_recv()
    tlse = [merged(rst, rb, t, n) for t in range(n)]

    mine = jnp.zeros((1, own), F32)
    for q in range(chips):
        mine = mine + jnp.where(chip == q, jnp.where(core == 0, ilse[q][:, :own], ilse[q][:, own:]), 0.0)
    for t in range(n):
        mine = mine + jnp.where(b == t, tlse[t], 0.0)
    pos = jnp.zeros((own, 2 * own), F32)
    slope = jnp.zeros((own, 2 * own), F32)
    line = lax.broadcasted_iota(jnp.int32, (own, 2 * own), 0)
    inverse = 1.0 / (2.0 * total)
    for t in range(n):
        low = to_column(tlse[t], diag)
        ids = line + (d * rows + t * own)
        for q in range(chips):
            y = lt[q, t]
            want = jnp.concatenate([pa[2 * q * n + b], pa[(2 * q + 1) * n + b]], axis=1)
            hit = ids == want
            w = (jnp.exp(y - low) + jnp.exp(y - ilse[q]) - jnp.where(hit, 2.0, 0.0)) * inverse
            pos = pos + jnp.where(hit, y, 0.0)
            slope = slope + w * y
            wl[q, t] = w.astype(BF)

    def whole(x):
        return jnp.sum(jnp.sum(x, axis=0, keepdims=True), axis=1, keepdims=True)

    loss = (whole(mine) - 2.0 * whole(pos)) * inverse
    scz[b, 0:1] = jnp.broadcast_to(loss, (1, 128))
    scz[b, 1:2] = jnp.broadcast_to(whole(slope), (1, 128))

    def text_up(t):
        y = nn(wl[0, t], pair(0))
        for q in range(1, chips):
            y = y + nn(wl[q, t], pair(q))
        return y

    tback = []
    for r in far:
        y, s = coded(text_up(zpeers[r]), 1)
        tq[r] = y
        ts[r] = to_lanes(s, diag)
        tback.append((r, post(tq.at[r], tqr.at[r], "branch", zpeers[r]), post(ts.at[r], tsr.at[r], "branch", zpeers[r])))
    zin = [post(scz.at[b], scz.at[b], "branch", zpeers[r]) for r in far]
    couple = []
    turn = list(range(1, chips)) + [0]
    for m in turn:
        k = xor(chip, m)
        y = tn(wl[k].reshape(rows, 2 * own), texts)
        iup[0, k] = y[:own]
        iup[1, k] = y[own:]
        couple.append(post(iup.at[other, k], crecv.at[k], "dp", dpeers[1]))
    raw[0] = text_up(b)
    iback = []
    for m, cp in zip(turn, couple):
        k = xor(chip, m)
        cp.wait_recv()
        y = iup[core, k] + crecv[k]
        if m:
            y, s = coded(y, 1)
            iq[m] = y
            isc[m] = to_lanes(s, diag)
            iback.append((m, post(iq.at[m], iqr.at[m], "dp", dpeers[2 * m]), post(isc.at[m], isr.at[m], "dp", dpeers[2 * m])))
        else:
            raw[1] = y

    def lower(up, u, size):
        radial = jnp.sum(up * u, axis=1, keepdims=True)
        return ((up - u * radial) / size).astype(BF)

    def spread(low, held, gathered):
        held[0] = low[:, :half]
        held[1] = low[:, half:]
        got = {}
        for m in outward + list(range(1, count, 2)):
            piece = core if m % 2 == 0 else other
            got[m] = post(held.at[piece], gathered.at[d], "dp", dpeers[m])
        gathered[d] = held[core]
        return got

    def hidden(low, proj, held, out):
        got = []
        for r in far:
            k = zpeers[r]
            held[r] = nt(low, proj[k]).astype(BF)
            got.append(post(held.at[r], out.at[b], "branch", k))
        out[b] = nt(low, proj[b]).astype(BF)
        return got

    def combined(up, back, codes, lengths):
        for r, cp, cq in back:
            cp.wait_recv()
            cq.wait_recv()
            up = up + decoded(codes[r]) * to_column(lengths[r], diag)
        return up

    low = lower(scale * combined(raw[1], iback, iqr, isr), iu[...], il[:, 0:1])
    igot = spread(low, di, dgi)
    ends = hidden(low, ip, ghi, oih)
    for cp in hin:
        cp.wait_recv()
    low = lower(scale * combined(raw[0], tback, tqr, tsr), tu[...], tl[:, 0:1])
    tgot = spread(low, dt, dgt)
    ends = ends + hidden(low, tp, ght, oth)

    def product(held, got, gathered, size, out):
        y = nn(held[d].reshape(n * size, own), gathered[d])
        for m in outward + list(range(1, count, 2)):
            got[m].wait_recv()
            y = y + nn(held[dpeers[m]].reshape(n * size, own), gathered[dpeers[m]])
        out[...] = y.reshape(n, size, half)

    def exchange(part, wp, held, came):
        got = []
        for r in far:
            y, s = coded(wp[zpeers[r]], 0)
            held[r] = y
            zs[part, r] = s
            got.append((r, post(held.at[r], came.at[r], "branch", zpeers[r]),
                        post(zs.at[part, r], zsr.at[part, r], "branch", zpeers[r])))
        return got

    def settle(part, wp, came, got, out):
        y = wp[b]
        for r, cp, cq in got:
            cp.wait_recv()
            cq.wait_recv()
            y = y + decoded(came[r]) * zsr[part, r]
        y, s = coded(y, 0)
        out[d] = y
        ws[part, d] = s
        got = {}
        for m in outward + [1]:
            got[m] = (post(out.at[d], out.at[d], "dp", dpeers[m]),
                      post(ws.at[part, d], ws.at[part, d], "dp", dpeers[m]))
        return got

    def relay(part, got, out):
        for m in outward:
            k = dpeers[m]
            for cp in got[m]:
                cp.wait_recv()
            got[m ^ 1] = (post(out.at[k], out.at[k], "dp", dpeers[1]),
                          post(ws.at[part, k], ws.at[part, k], "dp", dpeers[1]))

    product(hxg, igot, dgi, ri, wpi)
    iz = exchange(0, wpi, zqi, zqir)
    product(hyg, tgot, dgt, rt, wpt)
    tz = exchange(1, wpt, zqt, zqtr)
    for cp in zin:
        cp.wait_recv()
    y = scz[0]
    for s in range(1, n):
        y = y + scz[s]
    scd[d] = y
    din = [post(scd.at[d], scd.at[d], "dp", dpeers[m]) for m in range(1, count)]
    ilast = settle(0, wpi, zqir, iz, wqi)
    tlast = settle(1, wpt, zqtr, tz, wqt)
    relay(0, ilast, wqi)
    relay(1, tlast, wqt)
    for cp in din + ends:
        cp.wait_recv()
    y = scd[0]
    for s in range(1, count):
        y = y + scd[s]
    sc_out[...] = y
    for last in (ilast, tlast):
        for m in range(1, count, 2):
            for cp in last[m]:
                cp.wait_recv()
    post.finish()


def per_device(image_hidden, text_hidden, image_proj, text_proj, log_inverse_sharpness, partner):
    n = lax.axis_size("branch")
    count = lax.axis_size("dp")
    chips = count // 2
    group, wide = image_hidden.shape
    thin = text_hidden.shape[1]
    own = group // n
    embed = image_proj.shape[1]
    half = embed // 2
    ri, rt = wide // chips, thin // chips
    total = group * count
    spec = pl.BlockSpec(memory_space=VMEM)
    prows, pwidth = packed_shape(group, thin)
    outs = [((n, own, wide), BF), ((n, own, thin), BF), ((count, ri, half), I16), ((count, rt, half), I16),
            ((2, count, 1, half), F32), ((2, 128), F32)]
    scratch = [
        VMEM((n, own, wide), BF), VMEM((n, prows, pwidth), BF),
        VMEM((own, embed), F32), VMEM((own, 128), F32), VMEM((own, embed), F32), VMEM((own, 128), F32),
        VMEM((count, own, embed), BF), VMEM((n, own, embed), BF), VMEM((n, own, embed), F32),
        VMEM((chips, n, own, 2 * own), F32), VMEM((group, own), F32),
        VMEM((2, chips, 1, 2 * own), F32), VMEM((count, 2, chips, 1, 2 * own), F32),
        VMEM((2, n, 1, own), F32), VMEM((n, 2, n, 1, own), F32), VMEM((chips, n, own, 2 * own), BF),
        VMEM((n, own, embed), I16), VMEM((n, 1, own), F32), VMEM((n, own, embed), I16), VMEM((n, 1, own), F32),
        VMEM((2, chips, own, embed), F32), VMEM((chips, own, embed), F32),
        VMEM((chips, own, embed), I16), VMEM((chips, 1, own), F32), VMEM((chips, own, embed), I16), VMEM((chips, 1, own), F32),
        VMEM((chips, n, ri, own), BF), VMEM((chips, n, rt, own), BF),
        VMEM((count, n, ri, own), BF), VMEM((count, n, rt, own), BF),
        VMEM((2, own, half), BF), VMEM((2, own, half), BF), VMEM((count, own, half), BF), VMEM((count, own, half), BF),
        VMEM((n, own, wide), BF), VMEM((n, own, thin), BF),
        VMEM((n, ri, half), I16), VMEM((n, rt, half), I16), VMEM((n, ri, half), I16), VMEM((n, rt, half), I16),
        VMEM((2, n, 1, half), F32), VMEM((2, n, 1, half), F32), VMEM((n, ri, half), F32), VMEM((n, rt, half), F32),
        VMEM((n, 2, 128), F32), VMEM((count, 2, 128), F32),
        pltpu.SemaphoreType.DMA((2, 24 * n + 24 * count)),
    ]
    args = (
        image_hidden.reshape(n, own, wide), text_hidden,
        image_proj.reshape(n, wide, embed), text_proj.reshape(n, thin, embed),
        partner.reshape(count * n, 1, own), log_inverse_sharpness.reshape(1, 1),
    )
    gih, gth, wqi, wqt, ws, sc = pl.pallas_call(
        functools.partial(step_kernel, n, count, total),
        out_shape=[jax.ShapeDtypeStruct(s, t) for s, t in outs],
        in_specs=[spec] * len(args),
        out_specs=[spec] * len(outs),
        scratch_shapes=scratch,
        compiler_params=pltpu.CompilerParams(
            collective_id=0, has_side_effects=True, vmem_limit_bytes=60 * 1024 * 1024
        ),
    )(*args)

    def joined(codes, lengths, size):
        y = codes.astype(F32) * lengths
        y = y.reshape(chips, 2, size, half).transpose(0, 2, 1, 3)
        return y.reshape(chips * size, embed)

    return (
        sc[0, :1],
        sc[1, :1],
        gih.reshape(group, wide),
        gth.reshape(group, thin),
        joined(wqi, ws[0], ri),
        joined(wqt, ws[1], rt),
    )


def solution(mesh):
    placed = (P("dp", "branch"), P("dp", "branch"), P(), P(), P(), P())
    return jax.shard_map(
        per_device,
        mesh=mesh,
        in_specs=placed,
        out_specs=(
            P(),
            P(),
            P("dp", "branch"),
            P("dp", "branch"),
            P("branch", None),
            P("branch", None),
        ),
        check_vma=False,
    )
```

time: 169 us -> 98.9 us (0.59)
  Pallas kernels: 132 us -> 87.1 us
  matrix products: 18.3 us -> 0 us
  other arithmetic: 6.14 us -> 1.23 us
    pallas_call x4 -> x1, Pallas kernels: 132 us -> 87.1 us  [per_device(): pl.pallas_call(functools.partial(step_kernel, n, count, total), out_shape...]
    dot_general x7 -> x0, matrix products: 18.3 us -> none  [the longest x1 4.21 us: per_device(): ipart = scale * jnp.dot(low, text_emb, preferred_element_type=F32)]
    reduce_sum x3 -> x0, other arithmetic: 4.17 us -> none  [the longest x1 2.57 us: per_device(): scale_part = jnp.sum(weights * logits)]
    unnamed x13 -> x10, local copies, waits for them, and re-layouts: 5.77 us -> 6.02 us
where the time goes in v1:
time: 98.9 us; the launch traced here: 98.6 us
  Pallas kernels  87.1 us (88%)
  local copies, waits for them, and re-layouts  8.93 us (9%)
  between operations  1.34 us (1%)
  other arithmetic  1.23 us (1%)
    pallas_call x1, Pallas kernels, per_device(): pl.pallas_call(functools.partial(step_kernel, n, count, total), out_shape...  87.1 us
    unnamed x10, local copies, waits for them, and re-layouts  6.02 us

profile of v1, /device:TPU:0, one launch (start us, length us, event | category | flops | bytes accessed | tf_op | source)
XLA Modules:
  0.0 98.6 jit_solution(2579264334603291674)
XLA Ops:
  0.6 1.8 %copy.12.th = bf16[512,192]{1,0:T(8,128)(2,1)} copy(bf16[512,192]{0,1:T(8,128)(2,1)} %param.7) | data formatting | bytes 393216 | tf_op args[1]
  3.1 87.1 %shard_map.109 = (bf16[4,128,256]{2,1,0:T(8,128)(2,1)}, bf16[4,128,192]{2,1,0:T(8,128)(2,1)}, s16[8,64,384]{2,1,0:T(8,128)(2,1)}, s16[8,48,384]{2,1,0:T(8,128)(2...) custom-call(bf16[4,128,256]{2,1,0:T(8,128)(2,1)} %bitcast.36, bf16[512,192]{1,0:T(8,128)(2,1)} %copy.12.th, ...), custom_call_target="tpu_custom_call" | custom-call | tf_op jit(solution)/shard_map/pallas_call | solution.py:465
  90.1 1.3 %fusion.1 = (f32[1,1]{1,0:T(1,128)}, f32[1,1]{1,0:T(1,128)}) fusion(f32[2,128]{1,0:T(2,128)} %get-tuple-element.12), kind=kLoop, calls=%fused_computation.5 | loop fusion | bytes 16 | tf_op jit(solution)/shard_map/slice | solution.py:483
  91.4 1.8 %copy.15 = bf16[512,192]{0,1:T(8,128)(2,1)} copy(bf16[512,192]{1,0:T(8,128)(2,1)} %bitcast.34) | data formatting | bytes 393216
  93.2 0.7 fusion
  93.9 1.1 %convert_multiply_fusion = f32[8,64,384]{2,1,0:T(8,128)S(1)} fusion(s16[8,64,384]{2,1,0:T(8,128)(2,1)} %get-tuple-element.15, f32[8,384]{1,0:T(8,128)S(1)} %get-tuple-element.29), kind=kLoop, calls=%fused_computation | loop fusion | flops 393216 | bytes 1191936 | tf_op jit(solution)/shard_map/mul | solution.py:477
  95.0 0.0 copy-start
  95.0 0.6 copy.13
  95.7 0.9 copy.18
  96.6 0.0 copy-done
  96.6 0.0 copy-start.1
  96.6 0.1 convert_multiply_fusion.1
  96.7 0.3 copy.14
  97.0 0.9 copy.19
  97.9 0.0 copy-done.1
  97.9 0.7 copy.24
  (1 shorter events, 0.0 us)
Async XLA Ops:
  95.0 1.6 %copy-start = (s16[8,48,384]{2,1,0:T(8,128)(2,1)S(1)}, s16[8,48,384]{2,1,0:T(8,128)(2,1)}, u32[]{:S(2)}) copy-start(s16[8,48,384]{2,1,0:T(8,128)(2,1)} %get-tuple-element.17) | copy-start | bytes 884740
  96.6 1.3 %copy-start.1 = (bf16[4,128,256]{2,1,0:T(8,128)(2,1)S(1)}, bf16[4,128,256]{2,1,0:T(8,128)(2,1)}, u32[]{:S(2)}) copy-start(bf16[4,128,256]{2,1,0:T(8,128)(2,1)} %get-tuple-element.13) | copy-start | bytes 786436

commit v2 on v1

--- a/solution.py
+++ b/solution.py
@@ -44,8 +44,8 @@
     return lax.dot_general(a, b, (((0,), (0,)), ((), ())), preferred_element_type=F32)
 
 
-def eye(rows):
-    return lax.broadcasted_iota(jnp.int32, (rows, rows), 0) == lax.broadcasted_iota(jnp.int32, (rows, rows), 1)
+def eye(rows, lanes):
+    return lax.broadcasted_iota(jnp.int32, (rows, lanes), 0) == lax.broadcasted_iota(jnp.int32, (rows, lanes), 1)
 
 
 def to_lanes(column, diag):
@@ -85,15 +85,9 @@
             cp.wait_send()
 
 
-def packed_shape(rows, width):
-    if width == 192 and rows % 64 == 0:
-        return rows + rows // 2, 128
-    return rows, width
-
-
 def step_kernel(
     n, count, total, ih, th, ip, tp, pa, lg,
-    oih, oth, wqi, wqt, ws, sc_out,
+    oih, oth, wqi, wqt, wsi, wst, sc_out,
     xi, xt, iu, il, tu, tl, gi, temb, raw, lt, mx, cst, cb, rst, rb, wl,
     tq, ts, tqr, tsr, iup, crecv, iq, isc, iqr, isr, hx, hy, hxg, hyg, di, dt, dgi, dgt, ghi, ght,
     zqi, zqt, zqir, zqtr, zs, zsr, wpi, wpt, scz, scd, sems,
@@ -104,23 +98,22 @@
     chips = count // 2
     own, embed, width = ih.shape[1], ip.shape[2], tp.shape[1]
     rows, half = n * own, embed // 2
-    mid = rows // 2
+    hr = own // 2
     ri, rt = ip.shape[1] // chips, width // chips
-    packed = xt.shape[1] != rows
     post = Post(sems)
-    diag = eye(own)
+    diag = eye(own, own)
+    strip = eye(hr, own)
+    odds = list(range(n - 1, 1, -2))
+    evens = [r ^ 1 for r in odds]
+    start = pl.multiple_of(b * own, own)
+    column = pl.multiple_of(core * half, half)
     zpeers = [xor(b, r) for r in range(n)]
     dpeers = [xor(d, m) for m in range(count)]
     far = list(range(n - 1, 0, -1))
     outward = list(range(2, count, 2))
     bits = [1 << k for k in range(n.bit_length() - 1)][::-1]
 
-    if packed:
-        xt[b, :rows] = th[:, :128]
-        xt[b, rows:, :64] = th[:mid, 128:]
-        xt[b, rows:, 64:] = th[mid:, 128:]
-    else:
-        xt[b] = th[...]
+    xt[b] = th[...]
     greet([("branch", zpeers[r]) for r in range(1, n)] + [("dp", dpeers[m]) for m in range(1, count)])
 
     features = {r: post(ih.at[zpeers[r]], xi.at[b], "branch", zpeers[r]) for r in far}
@@ -148,17 +141,7 @@
         return x / size, size
 
     def text_part(s):
-        if packed:
-            main, tail = xt[s, :rows], xt[s, rows:]
-            low = tp[s, 128:, :]
-            zero = jnp.zeros_like(low)
-            y = nn(main, tp[s, :128, :])
-            lo = nn(tail, jnp.concatenate([low, zero], axis=0))
-            hi = nn(tail, jnp.concatenate([zero, low], axis=0))
-            y = y + jnp.concatenate([lo, hi], axis=0)
-        else:
-            y = nn(xt[s], tp[s])
-        return y.reshape(n, own, embed)
+        return tn(xt[s], tp[s]).reshape(n, own, embed)
 
     raw[...] = text_part(b)
     xi[b] = ih[b]
@@ -214,19 +197,11 @@
         rst[1, t] = to_lanes(jnp.sum(mass, axis=1, keepdims=True), diag)
     rin = [post(rst, rb.at[r], "branch", zpeers[r]) for r in far]
 
-    def turned(x):
-        return jnp.transpose(x.astype(F32))
-
-    start = pl.multiple_of(b * own, own)
     for s in range(n):
-        h = turned(xi[s]).astype(BF)
+        h = jnp.transpose(xi[s].astype(F32)).astype(BF)
         for q in range(chips):
             hx[q, s] = h[q * ri : (q + 1) * ri]
-        h = turned(xt[s, pl.ds(start, own)])
-        if packed:
-            tail = turned(xt[s, pl.ds(pl.multiple_of(rows + lax.rem(b, n // 2) * own, own), own)])
-            h = jnp.concatenate([h, jnp.where(b < n // 2, tail[:64], tail[64:])], axis=0)
-        h = h.astype(BF)
+        h = xt[s, :, pl.ds(start, own)]
         for q in range(chips):
             hy[q, s] = h[q * rt : (q + 1) * rt]
     hin = []
@@ -287,12 +262,24 @@
             y = y + nn(wl[q, t], pair(q))
         return y
 
-    tback = []
-    for r in far:
-        y, s = coded(text_up(zpeers[r]), 1)
-        tq[r] = y
-        ts[r] = to_lanes(s, diag)
-        tback.append((r, post(tq.at[r], tqr.at[r], "branch", zpeers[r]), post(ts.at[r], tsr.at[r], "branch", zpeers[r])))
+    def text_post(r, h, y, peer):
+        y, s = coded(y, 1)
+        tq[r, h] = y
+        ts[r, h] = to_lanes(s, strip)
+        return (post(tq.at[r, h], tqr.at[r, h], "branch", peer), post(ts.at[r, h], tsr.at[r, h], "branch", peer))
+
+    def text_take(r, h):
+        for cp in tback[(r, h)]:
+            cp.wait_recv()
+        return decoded(tqr[r, h]) * to_column(tsr[r, h], strip)
+
+    tback = {}
+    for r in odds:
+        y = text_up(zpeers[r])
+        for h in (0, 1):
+            tback[(r, h)] = text_post(r, h, y[h * hr : (h + 1) * hr], zpeers[1])
+    raw[1] = text_up(zpeers[1])
+    tback[(1, 0)] = text_post(1, 0, raw[1, :hr], zpeers[1])
     zin = [post(scz.at[b], scz.at[b], "branch", zpeers[r]) for r in far]
     couple = []
     turn = list(range(1, chips)) + [0]
@@ -303,6 +290,16 @@
         iup[1, k] = y[own:]
         couple.append(post(iup.at[other, k], crecv.at[k], "dp", dpeers[1]))
     raw[0] = text_up(b)
+    for e in evens:
+        raw[e] = text_up(zpeers[e])
+
+    def combine(h):
+        for e in evens:
+            y = raw[e, h * hr : (h + 1) * hr] + text_take(e ^ 1, h)
+            tback[(e, h)] = text_post(e, h, y, zpeers[e])
+
+    combine(0)
+    tback[(1, 1)] = text_post(1, 1, raw[1, hr:], zpeers[1])
     iback = []
     for m, cp in zip(turn, couple):
         k = xor(chip, m)
@@ -315,50 +312,59 @@
             iback.append((m, post(iq.at[m], iqr.at[m], "dp", dpeers[2 * m]), post(isc.at[m], isr.at[m], "dp", dpeers[2 * m])))
         else:
             raw[1] = y
+    combine(1)
 
     def lower(up, u, size):
         radial = jnp.sum(up * u, axis=1, keepdims=True)
         return ((up - u * radial) / size).astype(BF)
 
-    def spread(low, held, gathered):
-        held[0] = low[:, :half]
-        held[1] = low[:, half:]
-        got = {}
+    def spread(low, held, gathered, first, got):
+        size = low.shape[0]
+        held[0, first : first + size] = low[:, :half]
+        held[1, first : first + size] = low[:, half:]
         for m in outward + list(range(1, count, 2)):
             piece = core if m % 2 == 0 else other
-            got[m] = post(held.at[piece], gathered.at[d], "dp", dpeers[m])
-        gathered[d] = held[core]
-        return got
-
-    def hidden(low, proj, held, out):
-        got = []
-        for r in far:
-            k = zpeers[r]
-            held[r] = nt(low, proj[k]).astype(BF)
-            got.append(post(held.at[r], out.at[b], "branch", k))
-        out[b] = nt(low, proj[b]).astype(BF)
-        return got
-
-    def combined(up, back, codes, lengths):
-        for r, cp, cq in back:
-            cp.wait_recv()
-            cq.wait_recv()
-            up = up + decoded(codes[r]) * to_column(lengths[r], diag)
-        return up
-
-    low = lower(scale * combined(raw[1], iback, iqr, isr), iu[...], il[:, 0:1])
-    igot = spread(low, di, dgi)
-    ends = hidden(low, ip, ghi, oih)
+            cp = post(held.at[piece, pl.ds(first, size)], gathered.at[d, pl.ds(first, size)], "dp", dpeers[m])
+            got.setdefault(m, []).append(cp)
+        gathered[d, first : first + size] = held[core, first : first + size]
+
+    igot, tgot, ends = {}, {}, []
+
+    def text_half(h):
+        at = slice(h * hr, (h + 1) * hr)
+        up = raw[0, at]
+        for r in [1] + evens:
+            up = up + text_take(r, h)
+        spread(lower(scale * up, tu[at], tl[at, 0:1]), dt, dgt, h * hr, tgot)
+
+    text_half(0)
+    up = raw[1]
+    for m, cp, cq in iback:
+        cp.wait_recv()
+        cq.wait_recv()
+        up = up + decoded(iqr[m]) * to_column(isr[m], diag)
+    low = lower(scale * up, iu[...], il[:, 0:1])
+    spread(low, di, dgi, 0, igot)
+    for r in far:
+        k = zpeers[r]
+        ghi[r] = nt(low, ip[k]).astype(BF)
+        ends.append(post(ghi.at[r], oih.at[b], "branch", k))
+    oih[b] = nt(low, ip[b]).astype(BF)
     for cp in hin:
         cp.wait_recv()
-    low = lower(scale * combined(raw[0], tback, tqr, tsr), tu[...], tl[:, 0:1])
-    tgot = spread(low, dt, dgt)
-    ends = ends + hidden(low, tp, ght, oth)
+    text_half(1)
+    low = jnp.concatenate([dt[0], dt[1]], axis=1)
+    for r in far:
+        k = zpeers[r]
+        ght[r] = nt(tp[k], low).astype(BF)
+        ends.append(post(ght.at[r], oth.at[:, pl.ds(start, own)], "branch", k))
+    oth[:, pl.ds(start, own)] = nt(tp[b], low).astype(BF)
 
     def product(held, got, gathered, size, out):
         y = nn(held[d].reshape(n * size, own), gathered[d])
         for m in outward + list(range(1, count, 2)):
-            got[m].wait_recv()
+            for cp in got[m]:
+                cp.wait_recv()
             y = y + nn(held[dpeers[m]].reshape(n * size, own), gathered[dpeers[m]])
         out[...] = y.reshape(n, size, half)
 
@@ -379,21 +385,23 @@
             cq.wait_recv()
             y = y + decoded(came[r]) * zsr[part, r]
         y, s = coded(y, 0)
-        out[d] = y
-        ws[part, d] = s
+        out[chip, :, pl.ds(column, half)] = y
+        (wsi, wst)[part][chip, :, pl.ds(column, half)] = s
         got = {}
         for m in outward + [1]:
-            got[m] = (post(out.at[d], out.at[d], "dp", dpeers[m]),
-                      post(ws.at[part, d], ws.at[part, d], "dp", dpeers[m]))
+            got[m] = pass_on(part, chip, out, dpeers[m])
         return got
+
+    def pass_on(part, k, out, peer):
+        piece = out.at[k, :, pl.ds(column, half)]
+        lengths = (wsi, wst)[part].at[k, :, pl.ds(column, half)]
+        return (post(piece, piece, "dp", peer), post(lengths, lengths, "dp", peer))
 
     def relay(part, got, out):
         for m in outward:
-            k = dpeers[m]
             for cp in got[m]:
                 cp.wait_recv()
-            got[m ^ 1] = (post(out.at[k], out.at[k], "dp", dpeers[1]),
-                          post(ws.at[part, k], ws.at[part, k], "dp", dpeers[1]))
+            got[m ^ 1] = pass_on(part, xor(chip, m // 2), out, dpeers[1])
 
     product(hxg, igot, dgi, ri, wpi)
     iz = exchange(0, wpi, zqi, zqir)
@@ -421,6 +429,7 @@
             for cp in last[m]:
                 cp.wait_recv()
     post.finish()
+    assert post.count == sems.shape[1]
 
 
 def per_device(image_hidden, text_hidden, image_proj, text_proj, log_inverse_sharpness, partner):
@@ -435,34 +444,35 @@
     ri, rt = wide // chips, thin // chips
     total = group * count
     spec = pl.BlockSpec(memory_space=VMEM)
-    prows, pwidth = packed_shape(group, thin)
-    outs = [((n, own, wide), BF), ((n, own, thin), BF), ((count, ri, half), I16), ((count, rt, half), I16),
-            ((2, count, 1, half), F32), ((2, 128), F32)]
+    messages = 15 * (n - 1) + 12 * (count - 1) + 3 * chips - 2
+    outs = [((n, own, wide), BF), ((thin, group), BF), ((chips, ri, embed), I16), ((chips, rt, embed), I16),
+            ((chips, 1, embed), F32), ((chips, 1, embed), F32), ((2, 128), F32)]
     scratch = [
-        VMEM((n, own, wide), BF), VMEM((n, prows, pwidth), BF),
+        VMEM((n, own, wide), BF), VMEM((n, thin, group), BF),
         VMEM((own, embed), F32), VMEM((own, 128), F32), VMEM((own, embed), F32), VMEM((own, 128), F32),
         VMEM((count, own, embed), BF), VMEM((n, own, embed), BF), VMEM((n, own, embed), F32),
         VMEM((chips, n, own, 2 * own), F32), VMEM((group, own), F32),
         VMEM((2, chips, 1, 2 * own), F32), VMEM((count, 2, chips, 1, 2 * own), F32),
         VMEM((2, n, 1, own), F32), VMEM((n, 2, n, 1, own), F32), VMEM((chips, n, own, 2 * own), BF),
-        VMEM((n, own, embed), I16), VMEM((n, 1, own), F32), VMEM((n, own, embed), I16), VMEM((n, 1, own), F32),
+        VMEM((n, 2, own // 2, embed), I16), VMEM((n, 2, 1, own), F32),
+        VMEM((n, 2, own // 2, embed), I16), VMEM((n, 2, 1, own), F32),
         VMEM((2, chips, own, embed), F32), VMEM((chips, own, embed), F32),
         VMEM((chips, own, embed), I16), VMEM((chips, 1, own), F32), VMEM((chips, own, embed), I16), VMEM((chips, 1, own), F32),
         VMEM((chips, n, ri, own), BF), VMEM((chips, n, rt, own), BF),
         VMEM((count, n, ri, own), BF), VMEM((count, n, rt, own), BF),
         VMEM((2, own, half), BF), VMEM((2, own, half), BF), VMEM((count, own, half), BF), VMEM((count, own, half), BF),
-        VMEM((n, own, wide), BF), VMEM((n, own, thin), BF),
+        VMEM((n, own, wide), BF), VMEM((n, thin, own), BF),
         VMEM((n, ri, half), I16), VMEM((n, rt, half), I16), VMEM((n, ri, half), I16), VMEM((n, rt, half), I16),
         VMEM((2, n, 1, half), F32), VMEM((2, n, 1, half), F32), VMEM((n, ri, half), F32), VMEM((n, rt, half), F32),
         VMEM((n, 2, 128), F32), VMEM((count, 2, 128), F32),
-        pltpu.SemaphoreType.DMA((2, 24 * n + 24 * count)),
+        pltpu.SemaphoreType.DMA((2, messages)),
     ]
     args = (
-        image_hidden.reshape(n, own, wide), text_hidden,
+        image_hidden.reshape(n, own, wide), text_hidden.T,
         image_proj.reshape(n, wide, embed), text_proj.reshape(n, thin, embed),
         partner.reshape(count * n, 1, own), log_inverse_sharpness.reshape(1, 1),
     )
-    gih, gth, wqi, wqt, ws, sc = pl.pallas_call(
+    gih, gth, wqi, wqt, wsi, wst, sc = pl.pallas_call(
         functools.partial(step_kernel, n, count, total),
         out_shape=[jax.ShapeDtypeStruct(s, t) for s, t in outs],
         in_specs=[spec] * len(args),
@@ -473,18 +483,16 @@
         ),
     )(*args)
 
-    def joined(codes, lengths, size):
-        y = codes.astype(F32) * lengths
-        y = y.reshape(chips, 2, size, half).transpose(0, 2, 1, 3)
-        return y.reshape(chips * size, embed)
+    def joined(codes, lengths):
+        return (codes.astype(F32) * lengths).reshape(-1, embed)
 
     return (
         sc[0, :1],
         sc[1, :1],
         gih.reshape(group, wide),
-        gth.reshape(group, thin),
-        joined(wqi, ws[0], ri),
-        joined(wqt, ws[1], rt),
+        gth.T,
+        joined(wqi, wsi),
+        joined(wqt, wst),
     )
 
 

time: 98.9 us -> 91.9 us (0.929)
  local copies, waits for them, and re-layouts: 8.93 us -> 3.38 us
  Pallas kernels: 87.1 us -> 82.9 us
  other arithmetic: 1.23 us -> 3.88 us
    pallas_call x1, Pallas kernels: 87.1 us -> 82.9 us  [per_device(): pl.pallas_call(functools.partial(step_kernel, n, count, total), out_shape...]
    unnamed x10 -> x7, local copies, waits for them, and re-layouts: 6.02 us -> 2.12 us
    mul x2, other arithmetic: 1.23 us -> 3.88 us  [joined(): return (codes.astype(F32) * lengths).reshape(-1, embed)]
where the time goes in v2:
time: 91.9 us; the launch traced here: 91.5 us
  Pallas kernels  82.9 us (90%)
  other arithmetic  3.88 us (4%)
  local copies, waits for them, and re-layouts  3.38 us (4%)
  between operations  1.31 us (1%)
    pallas_call x1, Pallas kernels, per_device(): pl.pallas_call(functools.partial(step_kernel, n, count, total), out_shape...  82.9 us
    mul x2, other arithmetic, joined(): return (codes.astype(F32) * lengths).reshape(-1, embed)  3.88 us
    unnamed x7, local copies, waits for them, and re-layouts  2.12 us

profile of v2, /device:TPU:0, one launch (start us, length us, event | category | flops | bytes accessed | tf_op | source)
XLA Modules:
  0.0 91.5 jit_solution(17943655692270669810)
XLA Ops:
  1.3 82.9 %shard_map.109 = (bf16[4,128,256]{2,1,0:T(8,128)(2,1)}, bf16[192,512]{1,0:T(8,128)(2,1)}, s16[4,64,768]{2,1,0:T(8,128)(2,1)}, s16[4,48,768]{2,1,0:T(8,128)(2,1)}...) custom-call(bf16[4,128,256]{2,1,0:T(8,128)(2,1)} %bitcast.22, bf16[192,512]{1,0:T(8,128)(2,1)} %bitcast.24, ...), custom_call_target="tpu_custom_call" | custom-call | tf_op jit(solution)/shard_map/pallas_call | solution.py:475
  84.2 0.0 copy-start
  84.2 0.0 copy-start.1
  84.2 1.3 %fusion = (f32[1,1]{1,0:T(1,128)}, f32[1,1]{1,0:T(1,128)}) fusion(f32[2,128]{1,0:T(2,128)} %get-tuple-element.13), kind=kLoop, calls=%fused_computation.4 | loop fusion | bytes 16 | tf_op jit(solution)/shard_map/slice | solution.py:491
  85.5 0.7 copy_bitcast_fusion
  86.2 2.0 %convert_multiply_fusion = f32[4,64,768]{2,1,0:T(8,128)} fusion(s16[4,64,768]{2,1,0:T(8,128)(2,1)} %get-tuple-element.16, f32[4,768]{1,0:T(4,128)S(1)} %get-tuple-element.23), kind=kLoop, calls=%fused_computation | loop fusion | flops 393216 | bytes 1191936 | tf_op jit(solution)/shard_map/mul | solution.py:487
  88.2 1.9 %convert_multiply_fusion.1 = f32[4,48,768]{2,1,0:T(8,128)} fusion(s16[4,48,768]{2,1,0:T(8,128)(2,1)} %get-tuple-element.18, f32[4,768]{1,0:T(4,128)S(1)} %get-tuple-element.22), kind=kLoop, calls=%fused_computation.1 | loop fusion | flops 294912 | bytes 897024 | tf_op jit(solution)/shard_map/mul | solution.py:487
  90.1 0.0 copy-done
  90.1 0.7 copy.19
  90.8 0.0 copy-done.1
  90.8 0.7 copy.20
Async XLA Ops:
  84.2 5.9 %copy-start = (bf16[4,128,256]{2,1,0:T(8,128)(2,1)S(1)}, bf16[4,128,256]{2,1,0:T(8,128)(2,1)}, u32[]{:S(2)}) copy-start(bf16[4,128,256]{2,1,0:T(8,128)(2,1)} %get-tuple-element.14) | copy-start | bytes 786436
  84.2 6.6 %copy-start.1 = (bf16[192,512]{1,0:T(8,128)(2,1)S(1)}, bf16[192,512]{1,0:T(8,128)(2,1)}, u32[]{:S(2)}) copy-start(bf16[192,512]{1,0:T(8,128)(2,1)} %get-tuple-element.15) | copy-start | bytes 589828

commit v3 on v2

--- a/solution.py
+++ b/solution.py
@@ -86,11 +86,11 @@
 
 
 def step_kernel(
-    n, count, total, ih, th, ip, tp, pa, lg,
+    n, count, total, ih, th, ip_in, tp_in, pa, lg,
     oih, oth, wqi, wqt, wsi, wst, sc_out,
     xi, xt, iu, il, tu, tl, gi, temb, raw, lt, mx, cst, cb, rst, rb, wl,
     tq, ts, tqr, tsr, iup, crecv, iq, isc, iqr, isr, hx, hy, hxg, hyg, di, dt, dgi, dgt, ghi, ght,
-    zqi, zqt, zqir, zqtr, zs, zsr, wpi, wpt, scz, scd, sems,
+    zqi, zqt, zqir, zqtr, zs, zsr, wpi, wpt, scz, scd, ip, tp, loads, sems,
 ):
     b, d = lax.axis_index("branch"), lax.axis_index("dp")
     core, chip = lax.rem(d, 2), lax.div(d, 2)
@@ -113,37 +113,43 @@
     outward = list(range(2, count, 2))
     bits = [1 << k for k in range(n.bit_length() - 1)][::-1]
 
+    fetch = [pltpu.make_async_copy(ip_in, ip, loads.at[0]), pltpu.make_async_copy(tp_in, tp, loads.at[1])]
+    for cp in fetch:
+        cp.start()
     xt[b] = th[...]
     greet([("branch", zpeers[r]) for r in range(1, n)] + [("dp", dpeers[m]) for m in range(1, count)])
 
     features = {r: post(ih.at[zpeers[r]], xi.at[b], "branch", zpeers[r]) for r in far}
     parts = 2
-    prow = xt.shape[1] // parts
+    span = rows // parts
+    per = n // parts
     tin = {}
 
     def text_send(r, m, k):
-        piece = xt.at[zpeers[r], pl.ds(k * prow, prow)]
+        piece = xt.at[zpeers[r], :, pl.ds(k * span, span)]
         tin[(r ^ m, k)] = post(piece, piece, "branch", zpeers[m])
 
-    for m in bits:
-        for k in range(parts):
+    for k in range(parts):
+        for m in bits:
             text_send(0, m, k)
 
-    def arrive(r):
-        for k in range(parts):
-            tin[(r, k)].wait_recv()
-            for m in bits:
-                if m < (r & -r):
-                    text_send(r, m, k)
+    def arrive(r, k):
+        tin[(r, k)].wait_recv()
+        for m in bits:
+            if m < (r & -r):
+                text_send(r, m, k)
 
     def normal(x):
         size = jnp.sqrt(jnp.sum(x * x, axis=1, keepdims=True) + NORM_EPSILON)
         return x / size, size
 
-    def text_part(s):
-        return tn(xt[s], tp[s]).reshape(n, own, embed)
-
-    raw[...] = text_part(b)
+    def text_part(s, k):
+        return tn(xt[s, :, k * span : (k + 1) * span], tp[s]).reshape(per, own, embed)
+
+    for cp in fetch:
+        cp.wait()
+    for k in range(parts):
+        raw[k * per : (k + 1) * per] = text_part(b, k)
     xi[b] = ih[b]
     x = nn(ih[b], ip[b])
     for r in far[::-1]:
@@ -155,37 +161,75 @@
     gi[d] = u.astype(BF)
     gin = {m: post(gi.at[d], gi.at[d], "dp", dpeers[m]) for m in outward + [1]}
 
+    def pieces(held, gathered):
+        got = {}
+        for m in outward + [1]:
+            got[m] = post(held.at[xor(chip, m // 2)], gathered.at[d], "dp", dpeers[m])
+        gathered[d] = held[chip]
+        return got
+
+    def hand_over(got, gathered):
+        for m in outward:
+            got[m].wait_recv()
+            piece = gathered.at[dpeers[m]]
+            got[m ^ 1] = post(piece, piece, "dp", dpeers[1])
+
+    for s in range(n):
+        h = jnp.transpose(xi[s].astype(F32)).astype(BF)
+        for q in range(chips):
+            hx[q, s] = h[q * ri : (q + 1) * ri]
+    hin = pieces(hx, hxg)
+
+    def pair(q):
+        return gi[2 * q : 2 * q + 2].reshape(2 * own, embed)
+
+    scale = jnp.exp(lg[...])
+
+    def logits(k):
+        texts = temb[k * per : (k + 1) * per].reshape(span, embed)
+        for q in range(chips):
+            y = scale * nt(texts, pair(q))
+            lt[q, k * per : (k + 1) * per] = y.reshape(per, own, 2 * own)
+            near = jnp.maximum(y[:, :own], y[:, own:])
+            at = slice(k * span, (k + 1) * span)
+            mx[at] = near if q == 0 else jnp.maximum(mx[at], near)
+            top = jnp.max(y, axis=0, keepdims=True)
+            mass = jnp.sum(jnp.exp(y - top), axis=0, keepdims=True)
+            if k:
+                old = cst[0, q]
+                new = jnp.maximum(old, top)
+                mass = mass * jnp.exp(top - new) + cst[1, q] * jnp.exp(old - new)
+                top = new
+            cst[0, q] = top
+            cst[1, q] = mass
+
     arrival = sorted(range(1, n), key=lambda r: (r & 1, bin(r).count("1"), -r))
     for r in arrival:
-        if r == 1:
-            for m in outward:
+        if r & 1 == 0:
+            for k in range(parts):
+                arrive(r, k)
+            for k in range(parts):
+                at = slice(k * per, (k + 1) * per)
+                raw[at] = raw[at] + text_part(zpeers[r], k)
+    hand_over(gin, gi)
+    for k in range(parts):
+        at = slice(k * per, (k + 1) * per)
+        for r in arrival:
+            if r & 1:
+                arrive(r, k)
+                raw[at] = raw[at] + text_part(zpeers[r], k)
+        for t in range(k * per, (k + 1) * per):
+            u, _ = normal(raw[t])
+            temb[t] = u.astype(BF)
+        if k == 0:
+            hand_over(hin, hxg)
+            for m in range(1, count, 2):
                 gin[m].wait_recv()
-                piece = gi.at[dpeers[m]]
-                gin[m ^ 1] = post(piece, piece, "dp", dpeers[1])
-        arrive(r)
-        raw[...] = raw[...] + text_part(zpeers[r])
-    for t in range(n):
-        u, _ = normal(raw[t])
-        temb[t] = u.astype(BF)
+        logits(k)
     u, size = normal(raw[b])
     tu[...] = u
     tl[...] = jnp.broadcast_to(size, tl.shape)
-    for m in range(1, count, 2):
-        gin[m].wait_recv()
-
-    def pair(q):
-        return gi[2 * q : 2 * q + 2].reshape(2 * own, embed)
-
-    scale = jnp.exp(lg[...])
     texts = temb[...].reshape(rows, embed)
-    for q in range(chips):
-        y = scale * nt(texts, pair(q))
-        lt[q] = y.reshape(n, own, 2 * own)
-        top = jnp.max(y, axis=0, keepdims=True)
-        cst[0, q] = top
-        cst[1, q] = jnp.sum(jnp.exp(y - top), axis=0, keepdims=True)
-        near = jnp.maximum(y[:, :own], y[:, own:])
-        mx[...] = near if q == 0 else jnp.maximum(mx[...], near)
     cin = [post(cst, cb.at[m], "dp", dpeers[m]) for m in range(1, count)]
     for t in range(n):
         top = jnp.max(mx[pl.ds(t * own, own)], axis=1, keepdims=True)
@@ -198,19 +242,10 @@
     rin = [post(rst, rb.at[r], "branch", zpeers[r]) for r in far]
 
     for s in range(n):
-        h = jnp.transpose(xi[s].astype(F32)).astype(BF)
-        for q in range(chips):
-            hx[q, s] = h[q * ri : (q + 1) * ri]
         h = xt[s, :, pl.ds(start, own)]
         for q in range(chips):
             hy[q, s] = h[q * rt : (q + 1) * rt]
-    hin = []
-    for m in range(1, count):
-        k = lax.div(dpeers[m], 2)
-        hin.append(post(hx.at[k], hxg.at[d], "dp", dpeers[m]))
-        hin.append(post(hy.at[k], hyg.at[d], "dp", dpeers[m]))
-    hxg[d] = hx[chip]
-    hyg[d] = hy[chip]
+    yin = pieces(hy, hyg)
 
     def merged(held, came, k, many):
         top = held[0, k]
@@ -299,6 +334,7 @@
             tback[(e, h)] = text_post(e, h, y, zpeers[e])
 
     combine(0)
+    hand_over(yin, hyg)
     tback[(1, 1)] = text_post(1, 1, raw[1, hr:], zpeers[1])
     iback = []
     for m, cp in zip(turn, couple):
@@ -350,8 +386,9 @@
         ghi[r] = nt(low, ip[k]).astype(BF)
         ends.append(post(ghi.at[r], oih.at[b], "branch", k))
     oih[b] = nt(low, ip[b]).astype(BF)
-    for cp in hin:
-        cp.wait_recv()
+    for m in range(1, count, 2):
+        hin[m].wait_recv()
+        yin[m].wait_recv()
     text_half(1)
     low = jnp.concatenate([dt[0], dt[1]], axis=1)
     for r in far:
@@ -430,6 +467,15 @@
                 cp.wait_recv()
     post.finish()
     assert post.count == sems.shape[1]
+
+
+def output_kernel(gih, gth, wqi, wqt, wsi, wst, sc, loss, slope, oih, oth, oi, ot):
+    loss[...] = sc[0:1, 0:1]
+    slope[...] = sc[1:2, 0:1]
+    oih[...] = gih[...]
+    oth[...] = gth[...]
+    oi[...] = decoded(wqi[...]) * wsi[...]
+    ot[...] = decoded(wqt[...]) * wst[...]
 
 
 def per_device(image_hidden, text_hidden, image_proj, text_proj, log_inverse_sharpness, partner):
@@ -465,7 +511,8 @@
         VMEM((n, ri, half), I16), VMEM((n, rt, half), I16), VMEM((n, ri, half), I16), VMEM((n, rt, half), I16),
         VMEM((2, n, 1, half), F32), VMEM((2, n, 1, half), F32), VMEM((n, ri, half), F32), VMEM((n, rt, half), F32),
         VMEM((n, 2, 128), F32), VMEM((count, 2, 128), F32),
-        pltpu.SemaphoreType.DMA((2, messages)),
+        VMEM((n, wide, embed), BF), VMEM((n, thin, embed), BF),
+        pltpu.SemaphoreType.DMA((2,)), pltpu.SemaphoreType.DMA((2, messages)),
     ]
     args = (
         image_hidden.reshape(n, own, wide), text_hidden.T,
@@ -475,7 +522,7 @@
     gih, gth, wqi, wqt, wsi, wst, sc = pl.pallas_call(
         functools.partial(step_kernel, n, count, total),
         out_shape=[jax.ShapeDtypeStruct(s, t) for s, t in outs],
-        in_specs=[spec] * len(args),
+        in_specs=[spec, spec, pl.BlockSpec(memory_space=pl.ANY), pl.BlockSpec(memory_space=pl.ANY), spec, spec],
         out_specs=[spec] * len(outs),
         scratch_shapes=scratch,
         compiler_params=pltpu.CompilerParams(
@@ -483,16 +530,23 @@
         ),
     )(*args)
 
-    def joined(codes, lengths):
-        return (codes.astype(F32) * lengths).reshape(-1, embed)
-
+    loss, slope, oih, oth, oi, ot = pl.pallas_call(
+        output_kernel,
+        out_shape=[
+            jax.ShapeDtypeStruct((1, 1), F32), jax.ShapeDtypeStruct((1, 1), F32),
+            jax.ShapeDtypeStruct((n, own, wide), BF), jax.ShapeDtypeStruct((thin, group), BF),
+            jax.ShapeDtypeStruct((chips, ri, embed), F32), jax.ShapeDtypeStruct((chips, rt, embed), F32),
+        ],
+        in_specs=[spec] * 7,
+        out_specs=[spec] * 6,
+    )(gih, gth, wqi, wqt, wsi, wst, sc)
     return (
-        sc[0, :1],
-        sc[1, :1],
-        gih.reshape(group, wide),
-        gth.T,
-        joined(wqi, wsi),
-        joined(wqt, wst),
+        loss.reshape(1),
+        slope.reshape(1),
+        oih.reshape(group, wide),
+        oth.T,
+        oi.reshape(wide, embed),
+        ot.reshape(thin, embed),
     )
 
 

time: 91.9 us -> 86.7 us (0.943)
  other arithmetic: 3.88 us -> 0 us
  local copies, waits for them, and re-layouts: 3.38 us -> 0 us
  Pallas kernels: 82.9 us -> 85.1 us
    mul x2 -> x0, other arithmetic: 3.88 us -> none  [joined(): return (codes.astype(F32) * lengths).reshape(-1, embed)]
    pallas_call x0 -> x1, Pallas kernels: none -> 2.54 us  [per_device(): pl.pallas_call(output_kernel, out_shape=[jax.ShapeDtypeStruct((1, 1), F32...]
    unnamed x7 -> x0, local copies, waits for them, and re-layouts: 2.12 us -> none
    slice x1 -> x0, local copies, waits for them, and re-layouts: 1.26 us -> none  [per_device(): sc[1, :1]]
where the time goes in v3:
time: 86.7 us; the launch traced here: 86.4 us
  Pallas kernels  85.1 us (98%)
  between operations  1.29 us (1%)
    pallas_call x1, Pallas kernels, per_device(): pl.pallas_call(functools.partial(step_kernel, n, count, total), out_shape...  82.6 us
    pallas_call x1, Pallas kernels, per_device(): pl.pallas_call(output_kernel, out_shape=[jax.ShapeDtypeStruct((1, 1), F32...  2.54 us

profile of v3, /device:TPU:0, one launch (start us, length us, event | category | flops | bytes accessed | tf_op | source)
XLA Modules:
  0.0 86.4 jit_solution(18091988530263521540)
XLA Ops:
  1.3 82.6 %shard_map.109 = (bf16[4,128,256]{2,1,0:T(8,128)(2,1)}, bf16[192,512]{1,0:T(8,128)(2,1)}, s16[4,64,768]{2,1,0:T(8,128)(2,1)}, s16[4,48,768]{2,1,0:T(8,128)(2,1)}...) custom-call(bf16[4,128,256]{2,1,0:T(8,128)(2,1)} %bitcast.15, bf16[192,512]{1,0:T(8,128)(2,1)} %bitcast.16, ...), custom_call_target="tpu_custom_call" | custom-call | tf_op jit(solution)/shard_map/pallas_call | solution.py:522
  83.9 2.5 %shard_map.110 = (f32[1,1]{1,0:T(1,128)}, f32[1,1]{1,0:T(1,128)}, bf16[4,128,256]{2,1,0:T(8,128)(2,1)}, bf16[192,512]{1,0:T(8,128)(2,1)}, f32[4,64,768]{2,1,0:T(8,128)}, /*index=5*/f32[4,48,768]{2,1,0:T(8,128)}) custom-call(bf16[4,128,256]{2,1,0:T(8,128)(2,1)} %get-tuple-element.19.gih, bf16[192,512]{1,0:T(8,128)(2,1)} %get-tuple-element.20.gth, ...), custom_call_target="tpu_custom_call" | custom-call | tf_op jit(solution)/shard_map/pallas_call | solution.py:533

commit v4 on v3

--- a/solution.py
+++ b/solution.py
@@ -65,9 +65,13 @@
     return x.astype(jnp.int32).astype(F32)
 
 
+def ones(m):
+    return bin(m).count("1")
+
+
 class Post:
     def __init__(self, sems):
-        self.sems, self.count, self.sent = sems, 0, []
+        self.sems, self.count, self.sent, self.taken = sems, 0, [], set()
 
     def __call__(self, src, dst, axis, peer):
         i = self.count
@@ -79,6 +83,11 @@
         cp.start()
         self.sent.append(cp)
         return cp
+
+    def take(self, cp):
+        if id(cp) not in self.taken:
+            self.taken.add(id(cp))
+            cp.wait_recv()
 
     def finish(self):
         for cp in self.sent:
@@ -317,7 +326,8 @@
     tback[(1, 0)] = text_post(1, 0, raw[1, :hr], zpeers[1])
     zin = [post(scz.at[b], scz.at[b], "branch", zpeers[r]) for r in far]
     couple = []
-    turn = list(range(1, chips)) + [0]
+    turn = sorted(range(1, chips), key=lambda m: (ones(m) == 1, m)) + [0]
+    near = [m for m in range(1, chips) if ones(m) == 1]
     for m in turn:
         k = xor(chip, m)
         y = tn(wl[k].reshape(rows, 2 * own), texts)
@@ -336,51 +346,93 @@
     combine(0)
     hand_over(yin, hyg)
     tback[(1, 1)] = text_post(1, 1, raw[1, hr:], zpeers[1])
-    iback = []
+    iback = {}
+
+    def image_rows(m, h):
+        return iup[core, xor(chip, m), h * hr : (h + 1) * hr]
+
+    def image_post(m, h, y, via):
+        y, s = coded(y, 1)
+        iq[m, h] = y
+        isc[m, h] = to_lanes(s, strip)
+        iback[(m, h)] = (post(iq.at[m, h], iqr.at[m, h], "dp", dpeers[2 * via]),
+                         post(isc.at[m, h], isr.at[m, h], "dp", dpeers[2 * via]))
+
+    def image_take(m, h):
+        for cp in iback[(m, h)]:
+            cp.wait_recv()
+        return decoded(iqr[m, h]) * to_column(isr[m, h], strip)
+
+    def feeds(m, h):
+        return [x for x in near if (x < m if h == 0 else x > m)]
+
     for m, cp in zip(turn, couple):
         k = xor(chip, m)
         cp.wait_recv()
-        y = iup[core, k] + crecv[k]
-        if m:
-            y, s = coded(y, 1)
-            iq[m] = y
-            isc[m] = to_lanes(s, diag)
-            iback.append((m, post(iq.at[m], iqr.at[m], "dp", dpeers[2 * m]), post(isc.at[m], isr.at[m], "dp", dpeers[2 * m])))
-        else:
-            raw[1] = y
+        iup[core, k] = iup[core, k] + crecv[k]
+        for h in (0, 1):
+            if ones(m) == 2:
+                image_post(m, h, image_rows(m, h), m & -m if h == 0 else m ^ (m & -m))
+            elif ones(m) > 2 or (m and not feeds(m, h)):
+                image_post(m, h, image_rows(m, h), m)
     combine(1)
+    for m in near:
+        for h in (0, 1):
+            if feeds(m, h):
+                y = image_rows(m, h)
+                for x in feeds(m, h):
+                    y = y + image_take(m | x, h)
+                image_post(m, h, y, m)
 
     def lower(up, u, size):
         radial = jnp.sum(up * u, axis=1, keepdims=True)
         return ((up - u * radial) / size).astype(BF)
 
-    def spread(low, held, gathered, first, got):
+    def spread(low, held, gathered, first):
         size = low.shape[0]
         held[0, first : first + size] = low[:, :half]
         held[1, first : first + size] = low[:, half:]
-        for m in outward + list(range(1, count, 2)):
-            piece = core if m % 2 == 0 else other
-            cp = post(held.at[piece, pl.ds(first, size)], gathered.at[d, pl.ds(first, size)], "dp", dpeers[m])
-            got.setdefault(m, []).append(cp)
+        got = {}
+        for m in outward:
+            if ones(m) != 2:
+                for c in (0, 1):
+                    piece = held.at[core if c == 0 else other, pl.ds(first, size)]
+                    got[m | c] = [post(piece, gathered.at[d, pl.ds(first, size)], "dp", dpeers[m | c])]
+        piece = held.at[other, pl.ds(first, size)]
+        got[1] = [post(piece, gathered.at[d, pl.ds(first, size)], "dp", dpeers[1])]
         gathered[d, first : first + size] = held[core, first : first + size]
-
-    igot, tgot, ends = {}, {}, []
+        return got
+
+    def spread_on(got, gathered, first, size):
+        for c in (0, 1):
+            for m in outward:
+                if ones(m) == 2:
+                    one = m & -m
+                    for via, after, at in ((one, m ^ one, first), (m ^ one, one, first + size // 2)):
+                        post.take(got[via | c][0])
+                        piece = gathered.at[dpeers[via | c], pl.ds(at, size // 2)]
+                        got.setdefault(m | c, []).append(post(piece, piece, "dp", dpeers[after]))
+
+    ends = []
 
     def text_half(h):
         at = slice(h * hr, (h + 1) * hr)
         up = raw[0, at]
         for r in [1] + evens:
             up = up + text_take(r, h)
-        spread(lower(scale * up, tu[at], tl[at, 0:1]), dt, dgt, h * hr, tgot)
-
-    text_half(0)
-    up = raw[1]
-    for m, cp, cq in iback:
-        cp.wait_recv()
-        cq.wait_recv()
-        up = up + decoded(iqr[m]) * to_column(isr[m], diag)
-    low = lower(scale * up, iu[...], il[:, 0:1])
-    spread(low, di, dgi, 0, igot)
+        return spread(lower(scale * up, tu[at], tl[at, 0:1]), dt, dgt, h * hr)
+
+    tgot = [text_half(0)]
+    halves = []
+    for h in (0, 1):
+        up = image_rows(0, h)
+        for m in range(1, chips):
+            if ones(m) != 2:
+                up = up + image_take(m, h)
+        halves.append(up)
+    low = lower(scale * jnp.concatenate(halves, axis=0), iu[...], il[:, 0:1])
+    igot = spread(low, di, dgi, 0)
+    spread_on(tgot[0], dgt, 0, hr)
     for r in far:
         k = zpeers[r]
         ghi[r] = nt(low, ip[k]).astype(BF)
@@ -389,19 +441,22 @@
     for m in range(1, count, 2):
         hin[m].wait_recv()
         yin[m].wait_recv()
-    text_half(1)
+    tgot.append(text_half(1))
+    spread_on(igot, dgi, 0, own)
     low = jnp.concatenate([dt[0], dt[1]], axis=1)
     for r in far:
         k = zpeers[r]
         ght[r] = nt(tp[k], low).astype(BF)
         ends.append(post(ght.at[r], oth.at[:, pl.ds(start, own)], "branch", k))
     oth[:, pl.ds(start, own)] = nt(tp[b], low).astype(BF)
+    spread_on(tgot[1], dgt, hr, hr)
 
     def product(held, got, gathered, size, out):
         y = nn(held[d].reshape(n * size, own), gathered[d])
         for m in outward + list(range(1, count, 2)):
-            for cp in got[m]:
-                cp.wait_recv()
+            for part in got:
+                for cp in part[m]:
+                    post.take(cp)
             y = y + nn(held[dpeers[m]].reshape(n * size, own), gathered[dpeers[m]])
         out[...] = y.reshape(n, size, half)
 
@@ -440,7 +495,7 @@
                 cp.wait_recv()
             got[m ^ 1] = pass_on(part, xor(chip, m // 2), out, dpeers[1])
 
-    product(hxg, igot, dgi, ri, wpi)
+    product(hxg, [igot], dgi, ri, wpi)
     iz = exchange(0, wpi, zqi, zqir)
     product(hyg, tgot, dgt, rt, wpt)
     tz = exchange(1, wpt, zqt, zqtr)
@@ -452,8 +507,8 @@
     scd[d] = y
     din = [post(scd.at[d], scd.at[d], "dp", dpeers[m]) for m in range(1, count)]
     ilast = settle(0, wpi, zqir, iz, wqi)
+    relay(0, ilast, wqi)
     tlast = settle(1, wpt, zqtr, tz, wqt)
-    relay(0, ilast, wqi)
     relay(1, tlast, wqt)
     for cp in din + ends:
         cp.wait_recv()
@@ -490,7 +545,8 @@
     ri, rt = wide // chips, thin // chips
     total = group * count
     spec = pl.BlockSpec(memory_space=VMEM)
-    messages = 15 * (n - 1) + 12 * (count - 1) + 3 * chips - 2
+    twos = sum(ones(m) == 2 for m in range(chips))
+    messages = 15 * (n - 1) + 12 * (count - 1) + 5 * chips - 4 + 6 * twos
     outs = [((n, own, wide), BF), ((thin, group), BF), ((chips, ri, embed), I16), ((chips, rt, embed), I16),
             ((chips, 1, embed), F32), ((chips, 1, embed), F32), ((2, 128), F32)]
     scratch = [
@@ -503,7 +559,8 @@
         VMEM((n, 2, own // 2, embed), I16), VMEM((n, 2, 1, own), F32),
         VMEM((n, 2, own // 2, embed), I16), VMEM((n, 2, 1, own), F32),
         VMEM((2, chips, own, embed), F32), VMEM((chips, own, embed), F32),
-        VMEM((chips, own, embed), I16), VMEM((chips, 1, own), F32), VMEM((chips, own, embed), I16), VMEM((chips, 1, own), F32),
+        VMEM((chips, 2, own // 2, embed), I16), VMEM((chips, 2, 1, own), F32),
+        VMEM((chips, 2, own // 2, embed), I16), VMEM((chips, 2, 1, own), F32),
         VMEM((chips, n, ri, own), BF), VMEM((chips, n, rt, own), BF),
         VMEM((count, n, ri, own), BF), VMEM((count, n, rt, own), BF),
         VMEM((2, own, half), BF), VMEM((2, own, half), BF), VMEM((count, own, half), BF), VMEM((count, own, half), BF),

time: 86.7 us -> 88.5 us (1.021)
  Pallas kernels: 85.1 us -> 87 us
    pallas_call x1, Pallas kernels: 82.6 us -> 84.4 us  [per_device(): pl.pallas_call(functools.partial(step_kernel, n, count, total), out_shape...]
where the time goes in v4:
time: 88.5 us; the launch traced here: 88.3 us
  Pallas kernels  87 us (98%)
  between operations  1.29 us (1%)
    pallas_call x1, Pallas kernels, per_device(): pl.pallas_call(functools.partial(step_kernel, n, count, total), out_shape...  84.4 us
    pallas_call x1, Pallas kernels, per_device(): pl.pallas_call(output_kernel, out_shape=[jax.ShapeDtypeStruct((1, 1), F32...  2.54 us

profile of v4, /device:TPU:0, one launch (start us, length us, event | category | flops | bytes accessed | tf_op | source)
XLA Modules:
  0.0 88.3 jit_solution(6069677310842584706)
XLA Ops:
  1.3 84.4 %shard_map.109 = (bf16[4,128,256]{2,1,0:T(8,128)(2,1)}, bf16[192,512]{1,0:T(8,128)(2,1)}, s16[4,64,768]{2,1,0:T(8,128)(2,1)}, s16[4,48,768]{2,1,0:T(8,128)(2,1)}...) custom-call(bf16[4,128,256]{2,1,0:T(8,128)(2,1)} %bitcast.15, bf16[192,512]{1,0:T(8,128)(2,1)} %bitcast.16, ...), custom_call_target="tpu_custom_call" | custom-call | tf_op jit(solution)/shard_map/pallas_call | solution.py:579
  85.7 2.5 %shard_map.110 = (f32[1,1]{1,0:T(1,128)}, f32[1,1]{1,0:T(1,128)}, bf16[4,128,256]{2,1,0:T(8,128)(2,1)}, bf16[192,512]{1,0:T(8,128)(2,1)}, f32[4,64,768]{2,1,0:T(8,128)}, /*index=5*/f32[4,48,768]{2,1,0:T(8,128)}) custom-call(bf16[4,128,256]{2,1,0:T(8,128)(2,1)} %get-tuple-element.19.gih, bf16[192,512]{1,0:T(8,128)(2,1)} %get-tuple-element.20.gth, ...), custom_call_target="tpu_custom_call" | custom-call | tf_op jit(solution)/shard_map/pallas_call | solution.py:590

commit v5 on v3

--- a/solution.py
+++ b/solution.py
@@ -65,24 +65,48 @@
     return x.astype(jnp.int32).astype(F32)
 
 
+class Lot:
+    def __init__(self, post, span, both):
+        self.post, self.span = post, span
+        self.send = post.fresh()
+        self.recv = post.fresh() if both else None
+        post.lots.append(self)
+
+    def wait(self, i):
+        pltpu.make_async_copy(self.span, self.span, self.post.sems.at[i]).wait()
+
+    def wait_recv(self):
+        self.wait(self.recv)
+
+
 class Post:
     def __init__(self, sems):
-        self.sems, self.count, self.sent = sems, 0, []
-
-    def __call__(self, src, dst, axis, peer):
-        i = self.count
+        self.sems, self.count, self.sent, self.lots = sems, 0, [], []
+
+    def fresh(self):
         self.count += 1
+        return self.count - 1
+
+    def lot(self, span, both=False):
+        return Lot(self, span, both)
+
+    def __call__(self, src, dst, axis, peer, lot=None):
+        send = self.fresh() if lot is None else lot.send
+        recv = self.fresh() if lot is None or lot.recv is None else lot.recv
         cp = pltpu.make_async_remote_copy(
-            src_ref=src, dst_ref=dst, send_sem=self.sems.at[0, i], recv_sem=self.sems.at[1, i],
+            src_ref=src, dst_ref=dst, send_sem=self.sems.at[send], recv_sem=self.sems.at[recv],
             device_id={axis: peer}, device_id_type=MESH,
         )
         cp.start()
-        self.sent.append(cp)
+        if lot is None:
+            self.sent.append(cp)
         return cp
 
     def finish(self):
         for cp in self.sent:
             cp.wait_send()
+        for lot in self.lots:
+            lot.wait(lot.send)
 
 
 def step_kernel(
@@ -119,7 +143,9 @@
     xt[b] = th[...]
     greet([("branch", zpeers[r]) for r in range(1, n)] + [("dp", dpeers[m]) for m in range(1, count)])
 
-    features = {r: post(ih.at[zpeers[r]], xi.at[b], "branch", zpeers[r]) for r in far}
+    lot = post.lot(xi.at[: n - 1])
+    features = {r: post(ih.at[zpeers[r]], xi.at[b], "branch", zpeers[r], lot) for r in far}
+    text_lot = post.lot(xt.at[: n - 1])
     parts = 2
     span = rows // parts
     per = n // parts
@@ -127,7 +153,7 @@
 
     def text_send(r, m, k):
         piece = xt.at[zpeers[r], :, pl.ds(k * span, span)]
-        tin[(r ^ m, k)] = post(piece, piece, "branch", zpeers[m])
+        tin[(r ^ m, k)] = post(piece, piece, "branch", zpeers[m], text_lot)
 
     for k in range(parts):
         for m in bits:
@@ -159,26 +185,28 @@
     iu[...] = u
     il[...] = jnp.broadcast_to(size, il.shape)
     gi[d] = u.astype(BF)
-    gin = {m: post(gi.at[d], gi.at[d], "dp", dpeers[m]) for m in outward + [1]}
-
-    def pieces(held, gathered):
+    gin_lot = post.lot(gi.at[: count - 1])
+    gin = {m: post(gi.at[d], gi.at[d], "dp", dpeers[m], gin_lot) for m in outward + [1]}
+
+    def pieces(held, gathered, lot):
         got = {}
         for m in outward + [1]:
-            got[m] = post(held.at[xor(chip, m // 2)], gathered.at[d], "dp", dpeers[m])
+            got[m] = post(held.at[xor(chip, m // 2)], gathered.at[d], "dp", dpeers[m], lot)
         gathered[d] = held[chip]
         return got
 
-    def hand_over(got, gathered):
+    def hand_over(got, gathered, lot):
         for m in outward:
             got[m].wait_recv()
             piece = gathered.at[dpeers[m]]
-            got[m ^ 1] = post(piece, piece, "dp", dpeers[1])
+            got[m ^ 1] = post(piece, piece, "dp", dpeers[1], lot)
 
     for s in range(n):
         h = jnp.transpose(xi[s].astype(F32)).astype(BF)
         for q in range(chips):
             hx[q, s] = h[q * ri : (q + 1) * ri]
-    hin = pieces(hx, hxg)
+    hin_lot = post.lot(hxg.at[: count - 1])
+    hin = pieces(hx, hxg, hin_lot)
 
     def pair(q):
         return gi[2 * q : 2 * q + 2].reshape(2 * own, embed)
@@ -211,7 +239,7 @@
             for k in range(parts):
                 at = slice(k * per, (k + 1) * per)
                 raw[at] = raw[at] + text_part(zpeers[r], k)
-    hand_over(gin, gi)
+    hand_over(gin, gi, gin_lot)
     for k in range(parts):
         at = slice(k * per, (k + 1) * per)
         for r in arrival:
@@ -222,7 +250,7 @@
             u, _ = normal(raw[t])
             temb[t] = u.astype(BF)
         if k == 0:
-            hand_over(hin, hxg)
+            hand_over(hin, hxg, hin_lot)
             for m in range(1, count, 2):
                 gin[m].wait_recv()
         logits(k)
@@ -230,7 +258,9 @@
     tu[...] = u
     tl[...] = jnp.broadcast_to(size, tl.shape)
     texts = temb[...].reshape(rows, embed)
-    cin = [post(cst, cb.at[m], "dp", dpeers[m]) for m in range(1, count)]
+    cin = post.lot(cb.at[1:], True)
+    for m in range(1, count):
+        post(cst, cb.at[m], "dp", dpeers[m], cin)
     for t in range(n):
         top = jnp.max(mx[pl.ds(t * own, own)], axis=1, keepdims=True)
         mass = jnp.zeros((own, own), F32)
@@ -239,13 +269,16 @@
             mass = mass + e[:, :own] + e[:, own:]
         rst[0, t] = to_lanes(top, diag)
         rst[1, t] = to_lanes(jnp.sum(mass, axis=1, keepdims=True), diag)
-    rin = [post(rst, rb.at[r], "branch", zpeers[r]) for r in far]
+    rin = post.lot(rb.at[1:], True)
+    for r in far:
+        post(rst, rb.at[r], "branch", zpeers[r], rin)
 
     for s in range(n):
         h = xt[s, :, pl.ds(start, own)]
         for q in range(chips):
             hy[q, s] = h[q * rt : (q + 1) * rt]
-    yin = pieces(hy, hyg)
+    yin_lot = post.lot(hyg.at[: count - 1])
+    yin = pieces(hy, hyg, yin_lot)
 
     def merged(held, came, k, many):
         top = held[0, k]
@@ -256,11 +289,9 @@
             mass = mass + came[m, 1, k] * jnp.exp(came[m, 0, k] - top)
         return top + jnp.log(mass)
 
-    for cp in cin:
-        cp.wait_recv()
+    cin.wait_recv()
     ilse = [merged(cst, cb, q, count) for q in range(chips)]
-    for cp in rin:
-        cp.wait_recv()
+    rin.wait_recv()
     tlse = [merged(rst, rb, t, n) for t in range(n)]
 
     mine = jnp.zeros((1, own), F32)
@@ -308,6 +339,15 @@
             cp.wait_recv()
         return decoded(tqr[r, h]) * to_column(tsr[r, h], strip)
 
+    couple = []
+    couple_lot = post.lot(crecv)
+    turn = list(range(1, chips)) + [0]
+    for m in turn:
+        k = xor(chip, m)
+        y = tn(wl[k].reshape(rows, 2 * own), texts)
+        iup[0, k] = y[:own]
+        iup[1, k] = y[own:]
+        couple.append(post(iup.at[other, k], crecv.at[k], "dp", dpeers[1], couple_lot))
     tback = {}
     for r in odds:
         y = text_up(zpeers[r])
@@ -315,27 +355,9 @@
             tback[(r, h)] = text_post(r, h, y[h * hr : (h + 1) * hr], zpeers[1])
     raw[1] = text_up(zpeers[1])
     tback[(1, 0)] = text_post(1, 0, raw[1, :hr], zpeers[1])
-    zin = [post(scz.at[b], scz.at[b], "branch", zpeers[r]) for r in far]
-    couple = []
-    turn = list(range(1, chips)) + [0]
-    for m in turn:
-        k = xor(chip, m)
-        y = tn(wl[k].reshape(rows, 2 * own), texts)
-        iup[0, k] = y[:own]
-        iup[1, k] = y[own:]
-        couple.append(post(iup.at[other, k], crecv.at[k], "dp", dpeers[1]))
-    raw[0] = text_up(b)
-    for e in evens:
-        raw[e] = text_up(zpeers[e])
-
-    def combine(h):
-        for e in evens:
-            y = raw[e, h * hr : (h + 1) * hr] + text_take(e ^ 1, h)
-            tback[(e, h)] = text_post(e, h, y, zpeers[e])
-
-    combine(0)
-    hand_over(yin, hyg)
-    tback[(1, 1)] = text_post(1, 1, raw[1, hr:], zpeers[1])
+    zin = post.lot(scz.at[: n - 1], True)
+    for r in far:
+        post(scz.at[b], scz.at[b], "branch", zpeers[r], zin)
     iback = []
     for m, cp in zip(turn, couple):
         k = xor(chip, m)
@@ -347,44 +369,58 @@
             isc[m] = to_lanes(s, diag)
             iback.append((m, post(iq.at[m], iqr.at[m], "dp", dpeers[2 * m]), post(isc.at[m], isr.at[m], "dp", dpeers[2 * m])))
         else:
-            raw[1] = y
+            iup[core, k] = y
+    for e in evens:
+        raw[e] = text_up(zpeers[e])
+
+    def combine(h):
+        for e in evens:
+            y = raw[e, h * hr : (h + 1) * hr] + text_take(e ^ 1, h)
+            tback[(e, h)] = text_post(e, h, y, zpeers[e])
+
+    combine(0)
+    hand_over(yin, hyg, yin_lot)
+    tback[(1, 1)] = text_post(1, 1, raw[1, hr:], zpeers[1])
+    raw[0] = text_up(b)
     combine(1)
 
     def lower(up, u, size):
         radial = jnp.sum(up * u, axis=1, keepdims=True)
         return ((up - u * radial) / size).astype(BF)
 
-    def spread(low, held, gathered, first, got):
+    def spread(low, held, gathered, first, got, lot):
         size = low.shape[0]
         held[0, first : first + size] = low[:, :half]
         held[1, first : first + size] = low[:, half:]
         for m in outward + list(range(1, count, 2)):
             piece = core if m % 2 == 0 else other
-            cp = post(held.at[piece, pl.ds(first, size)], gathered.at[d, pl.ds(first, size)], "dp", dpeers[m])
+            cp = post(held.at[piece, pl.ds(first, size)], gathered.at[d, pl.ds(first, size)], "dp", dpeers[m], lot)
             got.setdefault(m, []).append(cp)
         gathered[d, first : first + size] = held[core, first : first + size]
 
-    igot, tgot, ends = {}, {}, []
+    igot, tgot = {}, {}
+    igot_lot, tgot_lot = post.lot(dgi.at[: count - 1]), post.lot(dgt.at[: count - 1])
+    ends = [post.lot(oih.at[: n - 1], True), post.lot(oth.at[:, : (n - 1) * own], True)]
 
     def text_half(h):
         at = slice(h * hr, (h + 1) * hr)
         up = raw[0, at]
         for r in [1] + evens:
             up = up + text_take(r, h)
-        spread(lower(scale * up, tu[at], tl[at, 0:1]), dt, dgt, h * hr, tgot)
+        spread(lower(scale * up, tu[at], tl[at, 0:1]), dt, dgt, h * hr, tgot, tgot_lot)
 
     text_half(0)
-    up = raw[1]
+    up = iup[core, chip]
     for m, cp, cq in iback:
         cp.wait_recv()
         cq.wait_recv()
         up = up + decoded(iqr[m]) * to_column(isr[m], diag)
     low = lower(scale * up, iu[...], il[:, 0:1])
-    spread(low, di, dgi, 0, igot)
+    spread(low, di, dgi, 0, igot, igot_lot)
     for r in far:
         k = zpeers[r]
         ghi[r] = nt(low, ip[k]).astype(BF)
-        ends.append(post(ghi.at[r], oih.at[b], "branch", k))
+        post(ghi.at[r], oih.at[b], "branch", k, ends[0])
     oih[b] = nt(low, ip[b]).astype(BF)
     for m in range(1, count, 2):
         hin[m].wait_recv()
@@ -394,7 +430,7 @@
     for r in far:
         k = zpeers[r]
         ght[r] = nt(tp[k], low).astype(BF)
-        ends.append(post(ght.at[r], oth.at[:, pl.ds(start, own)], "branch", k))
+        post(ght.at[r], oth.at[:, pl.ds(start, own)], "branch", k, ends[1])
     oth[:, pl.ds(start, own)] = nt(tp[b], low).astype(BF)
 
     def product(held, got, gathered, size, out):
@@ -444,19 +480,20 @@
     iz = exchange(0, wpi, zqi, zqir)
     product(hyg, tgot, dgt, rt, wpt)
     tz = exchange(1, wpt, zqt, zqtr)
-    for cp in zin:
-        cp.wait_recv()
+    zin.wait_recv()
     y = scz[0]
     for s in range(1, n):
         y = y + scz[s]
     scd[d] = y
-    din = [post(scd.at[d], scd.at[d], "dp", dpeers[m]) for m in range(1, count)]
+    din = post.lot(scd.at[: count - 1], True)
+    for m in range(1, count):
+        post(scd.at[d], scd.at[d], "dp", dpeers[m], din)
     ilast = settle(0, wpi, zqir, iz, wqi)
+    relay(0, ilast, wqi)
     tlast = settle(1, wpt, zqtr, tz, wqt)
-    relay(0, ilast, wqi)
     relay(1, tlast, wqt)
-    for cp in din + ends:
-        cp.wait_recv()
+    for lot in [din] + ends:
+        lot.wait_recv()
     y = scd[0]
     for s in range(1, count):
         y = y + scd[s]
@@ -466,7 +503,7 @@
             for cp in last[m]:
                 cp.wait_recv()
     post.finish()
-    assert post.count == sems.shape[1]
+    assert post.count == sems.shape[0], (post.count, sems.shape)
 
 
 def output_kernel(gih, gth, wqi, wqt, wsi, wst, sc, loss, slope, oih, oth, oi, ot):
@@ -490,7 +527,7 @@
     ri, rt = wide // chips, thin // chips
     total = group * count
     spec = pl.BlockSpec(memory_space=VMEM)
-    messages = 15 * (n - 1) + 12 * (count - 1) + 3 * chips - 2
+    messages = 20 + 19 * (n - 1) + 14 * (count - 1) + 5 * chips - 4
     outs = [((n, own, wide), BF), ((thin, group), BF), ((chips, ri, embed), I16), ((chips, rt, embed), I16),
             ((chips, 1, embed), F32), ((chips, 1, embed), F32), ((2, 128), F32)]
     scratch = [
@@ -512,7 +549,7 @@
         VMEM((2, n, 1, half), F32), VMEM((2, n, 1, half), F32), VMEM((n, ri, half), F32), VMEM((n, rt, half), F32),
         VMEM((n, 2, 128), F32), VMEM((count, 2, 128), F32),
         VMEM((n, wide, embed), BF), VMEM((n, thin, embed), BF),
-        pltpu.SemaphoreType.DMA((2,)), pltpu.SemaphoreType.DMA((2, messages)),
+        pltpu.SemaphoreType.DMA((2,)), pltpu.SemaphoreType.DMA((messages,)),
     ]
     args = (
         image_hidden.reshape(n, own, wide), text_hidden.T,

time: 86.7 us -> 85.8 us (0.990)
  no operation moved by 1% of the time
where the time goes in v5:
time: 85.8 us; the launch traced here: 85.6 us
  Pallas kernels  84.3 us (98%)
  between operations  1.29 us (2%)
    pallas_call x1, Pallas kernels, per_device(): pl.pallas_call(functools.partial(step_kernel, n, count, total), out_shape...  81.8 us
    pallas_call x1, Pallas kernels, per_device(): pl.pallas_call(output_kernel, out_shape=[jax.ShapeDtypeStruct((1, 1), F32...  2.54 us

profile of v5, /device:TPU:0, one launch (start us, length us, event | category | flops | bytes accessed | tf_op | source)
XLA Modules:
  0.0 85.6 jit_solution(12805370929228938040)
XLA Ops:
  1.3 81.8 %shard_map.109 = (bf16[4,128,256]{2,1,0:T(8,128)(2,1)}, bf16[192,512]{1,0:T(8,128)(2,1)}, s16[4,64,768]{2,1,0:T(8,128)(2,1)}, s16[4,48,768]{2,1,0:T(8,128)(2,1)}...) custom-call(bf16[4,128,256]{2,1,0:T(8,128)(2,1)} %bitcast.15, bf16[192,512]{1,0:T(8,128)(2,1)} %bitcast.16, ...), custom_call_target="tpu_custom_call" | custom-call | tf_op jit(solution)/shard_map/pallas_call | solution.py:559
  83.1 2.5 %shard_map.110 = (f32[1,1]{1,0:T(1,128)}, f32[1,1]{1,0:T(1,128)}, bf16[4,128,256]{2,1,0:T(8,128)(2,1)}, bf16[192,512]{1,0:T(8,128)(2,1)}, f32[4,64,768]{2,1,0:T(8,128)}, /*index=5*/f32[4,48,768]{2,1,0:T(8,128)}) custom-call(bf16[4,128,256]{2,1,0:T(8,128)(2,1)} %get-tuple-element.19.gih, bf16[192,512]{1,0:T(8,128)(2,1)} %get-tuple-element.20.gth, ...), custom_call_target="tpu_custom_call" | custom-call | tf_op jit(solution)/shard_map/pallas_call | solution.py:570

commit v6 on v5

--- a/solution.py
+++ b/solution.py
@@ -134,7 +134,7 @@
     zpeers = [xor(b, r) for r in range(n)]
     dpeers = [xor(d, m) for m in range(count)]
     far = list(range(n - 1, 0, -1))
-    outward = list(range(2, count, 2))
+    outward = sorted(range(2, count, 2), key=lambda m: -bin(m).count("1"))
     bits = [1 << k for k in range(n.bit_length() - 1)][::-1]
 
     fetch = [pltpu.make_async_copy(ip_in, ip, loads.at[0]), pltpu.make_async_copy(tp_in, tp, loads.at[1])]
@@ -341,7 +341,7 @@
 
     couple = []
     couple_lot = post.lot(crecv)
-    turn = list(range(1, chips)) + [0]
+    turn = [m // 2 for m in outward] + [0]
     for m in turn:
         k = xor(chip, m)
         y = tn(wl[k].reshape(rows, 2 * own), texts)
@@ -409,7 +409,6 @@
             up = up + text_take(r, h)
         spread(lower(scale * up, tu[at], tl[at, 0:1]), dt, dgt, h * hr, tgot, tgot_lot)
 
-    text_half(0)
     up = iup[core, chip]
     for m, cp, cq in iback:
         cp.wait_recv()
@@ -417,6 +416,7 @@
         up = up + decoded(iqr[m]) * to_column(isr[m], diag)
     low = lower(scale * up, iu[...], il[:, 0:1])
     spread(low, di, dgi, 0, igot, igot_lot)
+    text_half(0)
     for r in far:
         k = zpeers[r]
         ghi[r] = nt(low, ip[k]).astype(BF)
@@ -489,8 +489,8 @@
     for m in range(1, count):
         post(scd.at[d], scd.at[d], "dp", dpeers[m], din)
     ilast = settle(0, wpi, zqir, iz, wqi)
+    tlast = settle(1, wpt, zqtr, tz, wqt)
     relay(0, ilast, wqi)
-    tlast = settle(1, wpt, zqtr, tz, wqt)
     relay(1, tlast, wqt)
     for lot in [din] + ends:
         lot.wait_recv()

time: 85.8 us -> 85 us (level)
  no operation moved by 1% of the time
where the time goes in v6:
time: 85 us; the launch traced here: 84.8 us
  Pallas kernels  83.5 us (98%)
  between operations  1.29 us (2%)
    pallas_call x1, Pallas kernels, per_device(): pl.pallas_call(functools.partial(step_kernel, n, count, total), out_shape...  81 us
    pallas_call x1, Pallas kernels, per_device(): pl.pallas_call(output_kernel, out_shape=[jax.ShapeDtypeStruct((1, 1), F32...  2.54 us

profile of v6, /device:TPU:0, one launch (start us, length us, event | category | flops | bytes accessed | tf_op | source)
XLA Modules:
  0.0 84.8 jit_solution(736504723479671938)
XLA Ops:
  1.3 81.0 %shard_map.109 = (bf16[4,128,256]{2,1,0:T(8,128)(2,1)}, bf16[192,512]{1,0:T(8,128)(2,1)}, s16[4,64,768]{2,1,0:T(8,128)(2,1)}, s16[4,48,768]{2,1,0:T(8,128)(2,1)}...) custom-call(bf16[4,128,256]{2,1,0:T(8,128)(2,1)} %bitcast.15, bf16[192,512]{1,0:T(8,128)(2,1)} %bitcast.16, ...), custom_call_target="tpu_custom_call" | custom-call | tf_op jit(solution)/shard_map/pallas_call | solution.py:559
  82.3 2.5 %shard_map.110 = (f32[1,1]{1,0:T(1,128)}, f32[1,1]{1,0:T(1,128)}, bf16[4,128,256]{2,1,0:T(8,128)(2,1)}, bf16[192,512]{1,0:T(8,128)(2,1)}, f32[4,64,768]{2,1,0:T(8,128)}, /*index=5*/f32[4,48,768]{2,1,0:T(8,128)}) custom-call(bf16[4,128,256]{2,1,0:T(8,128)(2,1)} %get-tuple-element.19.gih, bf16[192,512]{1,0:T(8,128)(2,1)} %get-tuple-element.20.gth, ...), custom_call_target="tpu_custom_call" | custom-call | tf_op jit(solution)/shard_map/pallas_call | solution.py:570
